TPU v7x, 16 devices: a whole 2x2x2 slice. The times are simulated.
16 devices in a mesh: dp: 4 (over z, y), tp: 4 (over x, core).
Axes of the slice: x: 2, y: 2, z: 2, core: 2. Of those that a mesh axis runs over, the one named last changes fastest.
Arguments:
- hidden_in: bfloat16 [128, 2048], P('dp'), parts along dimension 0
- k_cache: bfloat16 [128, 256, 16, 128], P('dp', None, 'tp'), parts along dimension 0
- v_cache: bfloat16 [128, 256, 16, 128], P('dp', None, 'tp'), parts along dimension 0
- seq_lens: int32 [128], P('dp'), parts along dimension 0
- chosen_experts: int32 [128, 4], P('dp'), parts along dimension 0
- g_attn: bfloat16 [2048], replicated
- w_q: bfloat16 [2048, 2048], P(None, 'tp')
- w_k: bfloat16 [2048, 2048], P(None, 'tp')
- w_v: bfloat16 [2048, 2048], P(None, 'tp')
- w_o: bfloat16 [2048, 2048], P('tp')
- g_moe: bfloat16 [2048], replicated
- w_router: bfloat16 [2048, 60], replicated
- w_gate: bfloat16 [60, 2048, 1408], P(None, None, 'tp')
- w_up: bfloat16 [60, 2048, 1408], P(None, None, 'tp')
- w_down: bfloat16 [60, 1408, 2048], P(None, 'tp')
Outputs:
- output 1: bfloat16 [128, 2048], P('dp'), parts along dimension 0
- output 2: bfloat16 [128, 256, 16, 128], P('dp', None, 'tp'), parts along dimension 0
- output 3: bfloat16 [128, 256, 16, 128], P('dp', None, 'tp'), parts along dimension 0
There are 4 independent parts. A program takes and returns all parts, laid end to end along the dimension named above; an argument that names none is the same for every part.
All inputs are finite; a program needn't handle non-finite values.
Results may differ from a plain program's by a relative error of at most 0.0140183.
Values are sent between devices in bfloat16 or wider.
A program may use at most 1.25 GiB of HBM per device.

v0:
```python
import jax
import jax.numpy as jnp
from jax import lax
from jax.sharding import PartitionSpec as P

EPSILON = 1e-5
ROPE_THETA = 1000000.0
MASK_FILL = -1e30


def rms_norm(vector, gain_w):
    vector32 = vector.astype(jnp.float32)
    norm_scale = lax.rsqrt(jnp.mean(vector32 * vector32, axis=-1, keepdims=True) + EPSILON)
    return (vector32 * norm_scale * gain_w.astype(jnp.float32)).astype(jnp.bfloat16)


def rope_rotate(vector, cos_t, sin_t):
    half_dim = vector.shape[-1] // 2
    lead_half = vector[..., :half_dim]
    tail_half = vector[..., half_dim:]
    return jnp.concatenate([lead_half * cos_t - tail_half * sin_t, tail_half * cos_t + lead_half * sin_t], axis=-1)


def attention_part(hidden_in, k_cache, v_cache, seq_lens, g_attn, w_q, w_k, w_v):
    num_rows, num_slots, kv_heads, head_dim = k_cache.shape
    q_group = w_q.shape[1] // (head_dim * kv_heads)
    h_attn = rms_norm(hidden_in, g_attn)
    q_lin = jnp.dot(h_attn, w_q, preferred_element_type=jnp.float32).reshape(num_rows, kv_heads, q_group, head_dim)
    k_lin = jnp.dot(h_attn, w_k, preferred_element_type=jnp.float32).reshape(num_rows, kv_heads, head_dim)
    v_new = jnp.dot(h_attn, w_v, preferred_element_type=jnp.float32).reshape(num_rows, kv_heads, head_dim).astype(jnp.bfloat16)
    inv_freq = ROPE_THETA ** (-jnp.arange(0, head_dim, 2, dtype=jnp.float32) / head_dim)
    angles = seq_lens.astype(jnp.float32)[:, None] * inv_freq[None, :]
    cos_t = jnp.cos(angles)[:, None, :]
    sin_t = jnp.sin(angles)[:, None, :]
    q_rot = rope_rotate(q_lin, cos_t[:, :, None, :], sin_t[:, :, None, :]).astype(jnp.bfloat16)
    k_new = rope_rotate(k_lin, cos_t, sin_t).astype(jnp.bfloat16)
    slot_ids = jnp.arange(num_slots, dtype=jnp.int32)
    new_slot = (slot_ids[None, :] == seq_lens[:, None])[:, :, None, None]
    k_next = jnp.where(new_slot, k_new[:, None, :, :], k_cache)
    v_next = jnp.where(new_slot, v_new[:, None, :, :], v_cache)
    scores = jnp.einsum("bkgd,bskd->bkgs", q_rot, k_next, preferred_element_type=jnp.float32) * (head_dim ** -0.5)
    in_range = (slot_ids[None, :] <= seq_lens[:, None])[:, None, None, :]
    attn_weights = jax.nn.softmax(jnp.where(in_range, scores, MASK_FILL), axis=-1).astype(jnp.bfloat16)
    heads_out = jnp.einsum("bkgs,bskd->bkgd", attn_weights, v_next, preferred_element_type=jnp.float32)
    return heads_out.astype(jnp.bfloat16).reshape(num_rows, kv_heads * q_group * head_dim), k_next, v_next


def experts_part(hidden_mid, chosen_experts, g_moe, w_router, w_gate, w_up, w_down):
    num_experts = w_router.shape[1]
    h_moe = rms_norm(hidden_mid, g_moe)
    logits = jnp.dot(h_moe, w_router, preferred_element_type=jnp.float32)
    pick_mask = (chosen_experts[:, :, None] == jnp.arange(num_experts, dtype=jnp.int32)[None, None, :]).astype(jnp.float32)
    gate_probs = jax.nn.softmax(jnp.sum(pick_mask * logits[:, None, :], axis=-1), axis=-1)
    gate_mat = jnp.sum(gate_probs[:, :, None] * pick_mask, axis=1)
    up_gate = jnp.einsum("bd,edf->bef", h_moe, w_gate, preferred_element_type=jnp.float32)
    up_lin = jnp.einsum("bd,edf->bef", h_moe, w_up, preferred_element_type=jnp.float32)
    inner_act = (gate_mat[:, :, None] * jax.nn.silu(up_gate) * up_lin).astype(jnp.bfloat16)
    return jnp.einsum("bef,efd->bd", inner_act, w_down, preferred_element_type=jnp.float32)


def solution(mesh):
    cache_spec = P("dp", None, "tp", None)
    in_specs = (P("dp", None), cache_spec, cache_spec, P("dp"), P("dp", None), P(None), P(None, "tp"), P(None, "tp"), P(None, "tp"), P("tp", None), P(None), P(None, None), P(None, None, "tp"), P(None, None, "tp"), P(None, "tp", None))
    out_specs = (P("dp", None), cache_spec, cache_spec)

    def layer_shard(hidden_in, k_cache, v_cache, seq_lens, chosen_experts, g_attn, w_q, w_k, w_v, w_o, g_moe, w_router, w_gate, w_up, w_down):
        heads_out, k_next, v_next = attention_part(hidden_in, k_cache, v_cache, seq_lens, g_attn, w_q, w_k, w_v)
        attn_local = jnp.dot(heads_out, w_o, preferred_element_type=jnp.float32)
        attn_sum = lax.psum(attn_local, "tp")
        hidden_mid = (hidden_in.astype(jnp.float32) + attn_sum).astype(jnp.bfloat16)
        moe_local = experts_part(hidden_mid, chosen_experts, g_moe, w_router, w_gate, w_up, w_down)
        moe_sum = lax.psum(moe_local, "tp")
        hidden_out = (hidden_mid.astype(jnp.float32) + moe_sum).astype(jnp.bfloat16)
        return hidden_out, k_next, v_next

    return jax.shard_map(layer_shard, mesh=mesh, in_specs=in_specs, out_specs=out_specs, check_vma=False)
```

profile of v0, /device:TPU:0, one launch (start us, length us, event | category | flops | bytes accessed | tf_op | source)
XLA Modules:
  0.0 211.9 jit_solution(4734171052152186260)
XLA Ops:
  7.3 0.8 convert_element_type.63
  8.1 0.7 iota_compare_fusion.2
  8.8 1.0 fusion.13
  9.8 0.7 convert_element_type.61
  10.5 2.2 %convolution_convert_fusion = bf16[32,512]{1,0:T(8,128)(2,1)S(1)} fusion(bf16[2048,512]{1,0:T(8,128)(2,1)} %param.23, bf16[32,2048]{1,0:T(8,128)(2,1)} %param.15, f32[2048]{0:T(1024)S(1)} %convert_element_type.61, f32[32]{0:T(128)S(1)} %add_rsqrt_fusion.1), kind=kOutput, calls=%fused_computation.17 | convolution fusion | flops 67387392 | bytes 2269312 | tf_op jit(solution)/shard_map/dot_general | solution.py:30
  12.7 2.2 %fusion.49 = f32[32,512]{1,0:T(8,128)S(1)} fusion(bf16[2048,512]{1,0:T(8,128)(2,1)} %param.22, bf16[32,2048]{1,0:T(8,128)(2,1)} %param.15, f32[2048]{0:T(1024)S(1)} %convert_element_type.61, f32[32]{0:T(128)S(1)} %add_rsqrt_fusion.1), kind=kOutput, calls=%fused_computation.71 | convolution fusion | flops 67371008 | bytes 2302080 | tf_op jit(solution)/shard_map/dot_general | solution.py:29
  15.0 2.1 fusion.51
  17.1 0.1 multiply_cosine_fusion
  17.7 13.7 %broadcast_select_fusion.1 = (bf16[32,256,4,128]{3,2,1,0:T(4,128)(2,1)S(1)}, bf16[32,256,4,128]{3,2,1,0:T(4,128)(2,1)}) fusion(bf16[32,256,4,128]{3,2,1,0:T(4,128)(2,1)} %param.16, pred[32,256]{1,0:T(8,128)(4,1)S(1)} %get-tuple-element.14, bf16[32,4,128]{2,1,0:T(4,128)(2,1)S(1)} %pad_maximum_fusion, bf16[32,256,4,128]{3,2,1,0:T(4,128)(2,1)} %param.17, ...), kind=kLoop, calls=%fused_computation.7 | loop fusion | flops 8388608 | bytes 33628160 | tf_op jit(solution)/shard_map/jit(_where)/select_n | solution.py:39
  31.4 2.3 %fusion.4 = f32[32,4,1,256]{3,2,1,0:T(1,128)S(1)} fusion(bf16[32,256,4,128]{3,2,1,0:T(4,128)(2,1)S(1)} %get-tuple-element.9, bf16[32,4,128,1]{2,1,0,3:T(4,128)(2,1)S(1)} %maximum_bitcast_fusion), kind=kOutput, calls=%fused_computation.4 | convolution fusion | flops 8388608 | bytes 8552448 | tf_op jit(solution)/shard_map/bkgd,bskd->bkgs/dot_general | solution.py:41
  33.7 1.1 copy-done.1
  34.8 0.2 fusion.12
  35.0 4.6 %fusion.2 = f32[32,4,1,128]{3,2,1,0:T(1,128)S(1)} fusion(bf16[32,256,4,128]{3,2,1,0:T(4,128)(2,1)} %get-tuple-element.10, bf16[32,4,256,1]{2,0,1,3:T(8,128)(2,1)S(1)} %fusion.12), kind=kOutput, calls=%fused_computation.2 | convolution fusion | flops 8388608 | bytes 8519680 | tf_op jit(solution)/shard_map/bkgs,bskd->bkgd/dot_general | solution.py:44
  39.6 1.2 fusion.33
  40.8 0.2 all-reduce.5.cloned.1.call-start
  41.1 31.2 %all-reduce.3.cloned.1.call-done = f32[32,2048]{1,0:T(8,128)} async-done(((f32[32,2048]{1,0:T(8,128)}), f32[32,2048]{1,0:T(8,128)}) %all-reduce.3.cloned.1.call-update) | async-done | bytes 262160 | tf_op jit(solution)/shard_map/psum | solution.py:69
  72.2 1.1 fusion.17
  73.4 0.3 fusion.46
  73.6 0.2 select_reduce_fusion.1
  74.1 35.0 %fusion.21 = f32[32,60,352]{2,0,1:T(8,128)} fusion(bf16[60,2048,352]{1,2,0:T(8,128)(2,1)} %param.28, bf16[32,2048]{1,0:T(8,128)(2,1)S(1)} %get-tuple-element.4, f32[2048]{0:T(1024)S(1)} %convert_element_type.70, f32[32]{0:T(128)S(1)} %add_rsqrt_fusion), kind=kOutput, calls=%fused_computation.32 | convolution fusion | flops 2768502784 | bytes 89350272 | tf_op jit(solution)/shard_map/bd,edf->bef/dot_general | solution.py:56
  109.1 34.9 %multiply_convert_fusion.clone.4 = bf16[32,60,352]{2,0,1:T(8,128)(2,1)} fusion(f32[32,60,352]{2,0,1:T(8,128)} %fusion.21, bf16[60,2048,352]{1,2,0:T(8,128)(2,1)} %param.27, f32[32,60]{0,1:T(8,128)S(1)} %copy.19, bf16[32,2048]{1,0:T(8,128)(2,1)S(1)} %get-tuple-element.4, f32[2048]{0:T(1024)S(1)} %convert_element_type.70, ...), kind=kOutput, calls=%fused_computation.8.clone.clone.clone.1 | convolution fusion | flops 2773233664 | bytes 90709632 | tf_op jit(solution)/shard_map/bd,edf->bef/dot_general | solution.py:55
  144.0 30.8 %convolution_bitcast_fusion = f32[32,2048]{1,0:T(8,128)} fusion(bf16[60,352,2048]{2,1,0:T(8,128)(2,1)} %param.29, bf16[32,60,352]{2,0,1:T(8,128)(2,1)} %multiply_convert_fusion.clone.4), kind=kOutput, calls=%fused_computation.9 | convolution fusion | flops 2768240640 | bytes 88121344 | tf_op jit(solution)/shard_map/bef,efd->bd/dot_general | solution.py:58
  174.9 28.6 %all-reduce.5.cloned.1.call-done = f32[32,2048]{1,0:T(8,128)} async-done(((f32[32,2048]{1,0:T(8,128)}), f32[32,2048]{1,0:T(8,128)}) %all-reduce.5.cloned.1.call-update) | async-done | bytes 262160 | tf_op jit(solution)/shard_map/psum | solution.py:72
  203.4 1.6 fusion.20
  (31 shorter events, 0.9 us)
Async XLA Ops:
  7.2 32.5 %copy-start = (bf16[512,2048]{1,0:T(8,128)(2,1)S(1)}, bf16[512,2048]{1,0:T(8,128)(2,1)}, u32[]{:S(2)}) copy-start(bf16[512,2048]{1,0:T(8,128)(2,1)} %param.24) | copy-start | bytes 6291460
  7.2 7.8 %copy-start.2 = (bf16[32,2048]{1,0:T(8,128)(2,1)S(1)}, bf16[32,2048]{1,0:T(8,128)(2,1)}, u32[]{:S(2)}) copy-start(bf16[32,2048]{1,0:T(8,128)(2,1)} %param.15) | copy-start | bytes 393220
  7.2 65.0 %all-reduce.3.cloned.1.call-start = ((), (), s32[]{:S(2)}) async-start(), calls=%async_computation | async-start | bytes 524288 | tf_op jit(solution)/shard_map/psum | solution.py:69
  31.4 3.4 %copy-start.1 = (bf16[32,256,4,128]{3,2,1,0:T(4,128)(2,1)}, bf16[32,256,4,128]{3,2,1,0:T(4,128)(2,1)S(1)}, u32[]{:S(2)}) copy-start(bf16[32,256,4,128]{3,2,1,0:T(4,128)(2,1)S(1)} %get-tuple-element.9) | copy-start | bytes 25165828
  35.0 6.1 %copy-start.5 = (bf16[2048]{0:T(1024)(128)(2,1)S(1)}, bf16[2048]{0:T(1024)(128)(2,1)}, u32[]{:S(2)}) copy-start(bf16[2048]{0:T(1024)(128)(2,1)} %param.25) | copy-start | bytes 12292
  39.6 33.8 %copy-start.3 = (bf16[2048,60]{0,1:T(8,128)(2,1)S(1)}, bf16[2048,60]{0,1:T(8,128)(2,1)}, u32[]{:S(2)}) copy-start(bf16[2048,60]{0,1:T(8,128)(2,1)} %param.26) | copy-start | bytes 737284
  39.6 34.0 %copy-start.4 = (s32[32,4]{0,1:T(4,128)S(1)}, s32[32,4]{0,1:T(4,128)}, u32[]{:S(2)}) copy-start(s32[32,4]{0,1:T(4,128)} %param.19) | copy-start | bytes 1540
  40.8 162.6 %all-reduce.5.cloned.1.call-start = ((), (), s32[]{:S(2)}) async-start(), calls=%async_computation.1 | async-start | bytes 524288 | tf_op jit(solution)/shard_map/psum | solution.py:72
Sparse Core Ops, SparseCore 0:
  41.0 31.2 all-reduce.2
  175.0 28.3 all-reduce.4
where the time goes:
time: 213 us; the launch traced here: 212 us
  matrix products  115 us (54%)
  waiting for transfers between devices  59.7 us (28%)
  other arithmetic  20.9 us (10%)
  between operations  14.2 us (7%)
    dot_general x1, matrix products, experts_part(): jnp.einsum('bd,edf->bef', h_moe, w_up, preferred_element_type=jnp.float32)  35 us
    dot_general x1, matrix products, experts_part(): jnp.einsum('bd,edf->bef', h_moe, w_gate, preferred_element_type=jnp.float32)  34.9 us
    psum x1, waiting for transfers between devices, layer_shard(): attn_sum = lax.psum(attn_local, 'tp')  31.2 us
    dot_general x1, matrix products, experts_part(): jnp.einsum('bef,efd->bd', inner_act, w_down, preferred_element_type=jnp.f...  30.8 us
    psum x1, waiting for transfers between devices, layer_shard(): moe_sum = lax.psum(moe_local, 'tp')  28.6 us
    select_n x1, other arithmetic, attention_part(): k_next = jnp.where(new_slot, k_new[:, None, :, :], k_cache)  13.7 us
    dot_general x1, matrix products, attention_part(): jnp.einsum('bkgs,bskd->bkgd', attn_weights, v_next, preferred_element_typ...  4.57 us
  transfers between devices with their start and end apart: 2, of which 2 were waited for; matrix products, arithmetic and copies ran while one was open for 0% of the time, Pallas kernels for 0%

commit v1 on v0

v1 whole, which is shorter than its diff:
```python
import functools
import jax
import jax.numpy as jnp
from jax import lax
from jax.experimental import pallas as pl
from jax.experimental.pallas import tpu as pltpu
from jax.sharding import PartitionSpec as P

EPSILON = 1e-5
ROPE_THETA = 1000000.0
MASK_FILL = -1e30
MESH = pl.DeviceIdType.MESH
F32 = jnp.float32
BF16 = jnp.bfloat16
NT = (((1,), (1,)), ((), ()))
ANY = pl.BlockSpec(memory_space=pl.ANY)
VMEM = pl.BlockSpec(memory_space=pltpu.VMEM)
SMEM = pl.BlockSpec(memory_space=pltpu.SMEM)


def norm_rows(x32, gain):
    scale = lax.rsqrt(jnp.mean(x32 * x32, axis=-1, keepdims=True) + EPSILON)
    return (x32 * scale * gain.astype(F32)).astype(BF16)


def attention_kernel(lens, x_ref, g_ref, freq_ref, wq, wk, wv, wo, kc, vc, part_ref, kout, vout,
                     kbuf, vbuf, qkvw, wobuf, qs, ks, vs, os_, wsem, insem, outsem, *, group):
    rows = x_ref.shape[0]
    heads = wq.shape[1] // 128
    slots = kc.shape[1]
    steps = rows // group
    wcopies = [pltpu.make_async_copy(w, qkvw.at[i], wsem.at[i]) for i, w in enumerate((wq, wk, wv))]
    wocopy = pltpu.make_async_copy(wo, wobuf, wsem.at[3])
    for cp in wcopies:
        cp.start()

    def fetch(i, hbm, buf, j):
        at = pl.ds(i * group, group)
        return pltpu.make_async_copy(hbm.at[at], buf.at[at], insem.at[j, i])

    def flush(i, hbm, buf, j):
        at = pl.ds(i * group, group)
        return pltpu.make_async_copy(buf.at[at], hbm.at[at], outsem.at[j, i])

    for i in range(steps):
        fetch(i, kc, kbuf, 0).start()
        fetch(i, vc, vbuf, 1).start()
    wocopy.start()

    h = norm_rows(x_ref[...].astype(F32), g_ref[...])
    row_id = lax.broadcasted_iota(jnp.int32, (rows, 128), 0)
    pos = jnp.zeros((rows, 128), jnp.int32)
    for b in range(rows):
        pos = jnp.where(row_id == b, lens[b], pos)
    ang = pos.astype(F32) * freq_ref[...]
    cos_t = jnp.cos(ang)
    sin_t = jnp.sin(ang)
    lane = lax.broadcasted_iota(jnp.int32, (rows, 128), 1)
    sin_t = jnp.where(lane < 64, -sin_t, sin_t)

    def rope(u):
        return u * cos_t + pltpu.roll(u, 64, 1) * sin_t

    wcopies[0].wait()
    q = jnp.dot(h, qkvw[0], preferred_element_type=F32)
    wcopies[1].wait()
    k = jnp.dot(h, qkvw[1], preferred_element_type=F32)
    wcopies[2].wait()
    v = jnp.dot(h, qkvw[2], preferred_element_type=F32)
    for j in range(heads):
        cols = slice(128 * j, 128 * j + 128)
        qs[pl.ds(j, rows, stride=heads), :] = rope(q[:, cols]).astype(BF16).astype(F32)
        kj = rope(k[:, cols]).astype(BF16).astype(F32)
        vj = v[:, cols].astype(BF16).astype(F32)
        for rep in range(8 // heads):
            ks[pl.ds(j + rep * heads, rows, stride=8), :] = kj
            vs[pl.ds(j + rep * heads, rows, stride=8), :] = vj

    qrows = group * heads
    rid = lax.broadcasted_iota(jnp.int32, (qrows, slots), 0)
    cid = lax.broadcasted_iota(jnp.int32, (qrows, slots), 1)
    same_head = lax.rem(rid, heads) == lax.rem(cid, heads)
    slot = lax.div(cid, heads)
    seq_of = lax.div(rid, heads)
    oseq = lax.div(lax.broadcasted_iota(jnp.int32, (qrows, 128), 0), heads)
    trow = lax.div(lax.broadcasted_iota(jnp.int32, (16, 128), 0), heads)

    def insert(buf, new, b, p):
        at = pl.ds(pl.multiple_of(lax.div(p * heads, 16) * 16, 16), 16)
        n8 = new[pl.ds(pl.multiple_of(b * 8, 8), 8), :]
        n16 = jnp.concatenate([n8, n8], axis=0)
        old = buf[b, at, :].astype(F32)
        buf[b, at, :] = jnp.where(trow == lax.rem(p, 16 // heads), n16, old).astype(BF16)

    def step(i, carry):
        q16 = qs[pl.ds(pl.multiple_of(i * qrows, qrows), qrows), :].astype(BF16)
        fetch(i, kc, kbuf, 0).wait()
        ps = [lens[i * group + u] for u in range(group)]
        for u in range(group):
            insert(kbuf, ks, i * group + u, ps[u])
        flush(i, kout, kbuf, 0).start()
        sc = jnp.zeros((qrows, slots), F32)
        pm = jnp.zeros((qrows, slots), jnp.int32)
        for u in range(group):
            s_u = lax.dot_general(q16, kbuf[i * group + u], NT, preferred_element_type=F32)
            sc = jnp.where(seq_of == u, s_u, sc)
            pm = jnp.where(seq_of == u, ps[u], pm)
        sc = jnp.where(same_head & (slot <= pm), sc * (128 ** -0.5), MASK_FILL)
        ex = jnp.exp(sc - jnp.max(sc, axis=-1, keepdims=True))
        wt = (ex / jnp.sum(ex, axis=-1, keepdims=True)).astype(BF16)
        fetch(i, vc, vbuf, 1).wait()
        for u in range(group):
            insert(vbuf, vs, i * group + u, ps[u])
        flush(i, vout, vbuf, 1).start()
        o = jnp.zeros((qrows, 128), F32)
        for u in range(group):
            o_u = jnp.dot(wt, vbuf[i * group + u], preferred_element_type=F32)
            o = jnp.where(oseq == u, o_u, o)
        os_[pl.ds(pl.multiple_of(i * qrows, qrows), qrows), :] = o
        return carry

    lax.fori_loop(0, steps, step, 0)
    o = jnp.concatenate([os_[pl.ds(j, rows, stride=heads), :] for j in range(heads)], axis=1).astype(BF16)
    wocopy.wait()
    part_ref[...] = jnp.dot(o, wobuf[...], preferred_element_type=F32)

    def drain(i, carry):
        flush(i, kout, kbuf, 0).wait()
        flush(i, vout, vbuf, 1).wait()
        return carry

    lax.fori_loop(0, steps, drain, 0)


def attention(x, kc, vc, lens, g, wq, wk, wv, wo):
    rows, d_model = x.shape
    _, slots, _ = kc.shape
    width = wq.shape[1]
    heads = width // 128
    group = 4
    steps = rows // group
    freq = ROPE_THETA ** (-jnp.arange(0, 128, 2, dtype=F32) / 128)
    freq = jnp.concatenate([freq, freq])[None, :]
    return pl.pallas_call(
        functools.partial(attention_kernel, group=group),
        name="attention",
        out_shape=(jax.ShapeDtypeStruct((rows, d_model), F32),
                   jax.ShapeDtypeStruct(kc.shape, BF16), jax.ShapeDtypeStruct(vc.shape, BF16)),
        in_specs=[SMEM, VMEM, VMEM, VMEM, ANY, ANY, ANY, ANY, ANY, ANY],
        out_specs=(VMEM, ANY, ANY),
        scratch_shapes=[
            pltpu.VMEM((rows, slots, 128), BF16),
            pltpu.VMEM((rows, slots, 128), BF16),
            pltpu.VMEM((3, d_model, width), BF16),
            pltpu.VMEM((width, d_model), BF16),
            pltpu.VMEM((rows * heads, 128), F32),
            pltpu.VMEM((rows * 8, 128), F32),
            pltpu.VMEM((rows * 8, 128), F32),
            pltpu.VMEM((rows * heads, 128), F32),
            pltpu.SemaphoreType.DMA((4,)),
            pltpu.SemaphoreType.DMA((2, steps)),
            pltpu.SemaphoreType.DMA((2, steps)),
        ],
        compiler_params=pltpu.CompilerParams(vmem_limit_bytes=63 << 20),
        cost_estimate=pl.CostEstimate(flops=400_000_000, bytes_accessed=42_000_000, transcendentals=0),
    )(lens, x, g[None, :], freq, wq, wk, wv, wo, kc, vc)


def experts_kernel(part, x_ref, g_ref, picks, wr, wg, wu, wd, out_ref,
                   gbuf, ubuf, dbuf, xf, recv1, hall, hb, gall, z, acc, drecv, psum, frecv, yall,
                   gsem, usem, dsem, s1, r1, s2, r2, s3, r3, s4, r4, s5, r5, s6, r6, s7, r7, s8, r8,
                   *, n_dp, n_tp, ring, chunks):
    dp = lax.axis_index("dp")
    tp = lax.axis_index("tp")
    core = lax.rem(tp, 2)
    xx = lax.div(tp, 2)
    n_exp, f_dim, d_model = wg.shape
    mine = n_exp // n_dp
    base = dp * mine
    f_pad = z.shape[1] // mine
    n_chip = n_dp * n_tp // 2
    me_chip = dp * (n_tp // 2) + xx
    me = dp * n_tp + tp
    n_blk = n_dp * n_tp
    rows = x_ref.shape[0]
    cw = d_model // chunks

    def flip(v, bit):
        return 1 - v if bit else v

    def chip_peer(m):
        px = flip(xx, m & 1)
        pd = 2 * flip(lax.div(dp, 2), (m >> 2) & 1) + flip(lax.rem(dp, 2), (m >> 1) & 1)
        return pd, px

    peers = []
    for m in range(1, n_chip):
        pd, px = chip_peer(m)
        peers.append({"dp": pd, "tp": 2 * px + core})
    partner = {"dp": dp, "tp": 2 * xx + 1 - core}
    cross = {"dp": dp, "tp": 2 * (1 - xx) + 1 - core}

    def gcopy(e, s):
        return pltpu.make_async_copy(wg.at[base + e], gbuf.at[s], gsem.at[s])

    def ucopy(e, s):
        return pltpu.make_async_copy(wu.at[base + e], ubuf.at[s], usem.at[s])

    def dcopy(e):
        return pltpu.make_async_copy(wd.at[base + e], dbuf.at[pl.ds(e * f_pad, f_dim)], dsem.at[e])

    barrier = pltpu.get_barrier_semaphore()
    for dev in peers + [partner, cross]:
        pl.semaphore_signal(barrier, inc=1, device_id=dev, device_id_type=MESH)
    for e in range(ring):
        gcopy(e, e).start()
        ucopy(e, e).start()
    for e in range(mine):
        dcopy(e).start()
    xf[...] = x_ref[...].astype(F32)
    pl.semaphore_wait(barrier, len(peers) + 2)

    def block(t):
        return pl.ds(pl.multiple_of(t * 8, 8), 8)

    first = []
    for k in range(1, n_tp):
        t_to = lax.rem(tp + k, n_tp)
        cp = pltpu.make_async_remote_copy(
            src_ref=part.at[block(t_to)], dst_ref=recv1.at[k - 1],
            send_sem=s1.at[k - 1], recv_sem=r1.at[k - 1],
            device_id={"dp": dp, "tp": t_to}, device_id_type=MESH)
        cp.start()
        first.append(cp)

    for e in range(mine):
        dbuf[pl.ds(e * f_pad + f_dim, f_pad - f_dim), :] = jnp.zeros((f_pad - f_dim, d_model), BF16)
    z[...] = jnp.zeros_like(z)
    pick_cols = []
    row8 = lax.broadcasted_iota(jnp.int32, (8, 128), 0)
    for kk in range(picks.shape[0]):
        pc = jnp.zeros((8, 128), jnp.int32)
        for i in range(8):
            pc = jnp.where(row8 == i, picks[kk, tp * 8 + i], pc)
        pick_cols.append(pc)

    for cp in first:
        cp.wait()
    attn_sum = part[block(tp), :]
    for k in range(1, n_tp):
        attn_sum = attn_sum + recv1[k - 1]
    x1 = (xf[block(tp), :] + attn_sum).astype(BF16).astype(F32)
    xf[block(tp), :] = x1
    h2 = norm_rows(x1, g_ref[...])
    hall[me] = h2

    def spread(buf, i, m, ssem, rsem):
        return pltpu.make_async_remote_copy(
            src_ref=buf.at[i], dst_ref=buf.at[i], send_sem=ssem.at[m], recv_sem=rsem.at[m],
            device_id=peers[m], device_id_type=MESH)

    def relay(buf, i, m, ssem, rsem):
        return pltpu.make_async_remote_copy(
            src_ref=buf.at[i], dst_ref=buf.at[i], send_sem=ssem.at[m], recv_sem=rsem.at[m],
            device_id=partner, device_id_type=MESH)

    order = sorted(range(n_chip - 1), key=lambda m: -bin(m + 1).count("1"))
    hs = [spread(hall, me, m, s2, r2) for m in range(n_chip - 1)]
    hd = [relay(hall, me, n_chip - 1, s3, r3)]
    for m in order:
        hs[m].start()
    hd[0].start()

    logits = lax.dot_general(h2, wr[...], NT, preferred_element_type=F32)
    lane = lax.broadcasted_iota(jnp.int32, (8, 128), 1)
    picked = []
    for pc in pick_cols:
        hit = (lane == pc)[:, :n_exp]
        picked.append(jnp.sum(jnp.where(hit, logits, 0.0), axis=1, keepdims=True))
    top = functools.reduce(jnp.maximum, picked)
    exs = [jnp.exp(p - top) for p in picked]
    den = functools.reduce(lambda a, b: a + b, exs)
    gates = jnp.zeros((8, 128), F32)
    for pc, ex in zip(pick_cols, exs):
        gates = gates + jnp.where(lane == pc, ex / den, 0.0)
    gall[me] = gates
    gs = [spread(gall, me, m, s4, r4) for m in range(n_chip - 1)]
    gd = [relay(gall, me, n_chip - 1, s5, r5)]
    for m in order:
        gs[m].start()
    gd[0].start()

    def owner(m):
        pd, px = chip_peer(m + 1)
        return pd * n_tp + 2 * px + core

    for m in reversed(order):
        hs[m].wait_recv()
        cp = relay(hall, owner(m), m, s3, r3)
        cp.start()
        hd.append(cp)
    for m in reversed(order):
        gs[m].wait_recv()
        cp = relay(gall, owner(m), m, s5, r5)
        cp.start()
        gd.append(cp)
    for cp in hd + gd:
        cp.wait_recv()
    for cp in hs + gs + hd + gd:
        cp.wait_send()

    for r in range(n_blk // 2):
        two = jnp.concatenate([hall[2 * r].astype(F32), hall[2 * r + 1].astype(F32)], axis=0)
        hb[16 * r:16 * r + 16, :] = two.astype(BF16)
    gmat = gall[...].reshape(n_blk * 8, 128)
    glane = lax.broadcasted_iota(jnp.int32, (n_blk * 8, 128), 1)

    def expert(e, s):
        gcopy(e, s).wait()
        ucopy(e, s).wait()
        gate = lax.dot_general(hb[...], gbuf[s], NT, preferred_element_type=F32)
        up = lax.dot_general(hb[...], ubuf[s], NT, preferred_element_type=F32)
        gcol = jnp.sum(jnp.where(glane == base + e, gmat, 0.0), axis=1, keepdims=True)
        return (gcol * (gate * jax.nn.sigmoid(gate)) * up).astype(BF16)

    unroll = 3
    for e0 in range(0, mine, unroll):
        for e in range(e0, e0 + unroll):
            s = e % ring
            z[:, e * f_pad:e * f_pad + f_dim] = expert(e, s)
            if e + ring < mine:
                gcopy(e + ring, s).start()
                ucopy(e + ring, s).start()

    for e in range(mine):
        dcopy(e).wait()

    pend = []
    finals = {}
    pair = {}

    def pair_sum(n):
        pair[n].wait_recv()
        psum[n] = acc[n, core] + drecv[n]
        for m in order:
            pd, px = chip_peer(m + 1)
            chip = pd * (n_tp // 2) + px
            cp = pltpu.make_async_remote_copy(
                src_ref=psum.at[n, block(chip)], dst_ref=frecv.at[n, m],
                send_sem=s7.at[n, m], recv_sem=r7.at[n, m], device_id=peers[m], device_id_type=MESH)
            cp.start()
            finals[n, m] = cp

    for n in range(chunks):
        res = jnp.dot(z[...], dbuf[:, n * cw:(n + 1) * cw], preferred_element_type=F32)
        for j in range(n_chip):
            for q in range(2):
                at = (2 * j + q) * 8
                acc[n, q, 8 * j:8 * j + 8, :] = res[at:at + 8, :]
        cp = pltpu.make_async_remote_copy(
            src_ref=acc.at[n, 1 - core], dst_ref=drecv.at[n], send_sem=s6.at[n], recv_sem=r6.at[n],
            device_id=partner, device_id_type=MESH)
        cp.start()
        pair[n] = cp
        if n >= 1:
            pair_sum(n - 1)
    pair_sum(chunks - 1)
    for n in range(chunks):
        total = psum[n, block(me_chip), :]
        for m in range(n_chip - 1):
            finals[n, m].wait_recv()
            total = total + frecv[n, m]
        cols = slice(n * cw, (n + 1) * cw)
        yall[tp, :, cols] = (xf[block(tp), cols] + total).astype(BF16)
    last = []
    for k in range(1, n_tp):
        t_to = lax.rem(tp + k, n_tp)
        cp = pltpu.make_async_remote_copy(
            src_ref=yall.at[tp], dst_ref=yall.at[tp], send_sem=s8.at[k - 1], recv_sem=r8.at[k - 1],
            device_id={"dp": dp, "tp": t_to}, device_id_type=MESH)
        cp.start()
        last.append(cp)
    for cp in last:
        cp.wait_recv()
    out_ref[...] = yall[...]
    for cp in last + list(pair.values()) + list(finals.values()):
        cp.wait_send()


def experts(part, x, picks, g, wr, wg, wu, wd, n_dp, n_tp):
    rows, d_model = x.shape
    n_exp, f_dim, _ = wg.shape
    mine = n_exp // n_dp
    f_pad = -(-f_dim // 128) * 128
    ring, chunks = 10, 4
    n_chip = n_dp * n_tp // 2
    cw = d_model // chunks
    dma = pltpu.SemaphoreType.DMA
    out = pl.pallas_call(
        functools.partial(experts_kernel, n_dp=n_dp, n_tp=n_tp, ring=ring, chunks=chunks),
        name="experts",
        out_shape=jax.ShapeDtypeStruct((n_tp, 8, d_model), BF16),
        in_specs=[VMEM, VMEM, VMEM, SMEM, VMEM, ANY, ANY, ANY],
        out_specs=VMEM,
        scratch_shapes=[
            pltpu.VMEM((ring, f_dim, d_model), BF16),
            pltpu.VMEM((ring, f_dim, d_model), BF16),
            pltpu.VMEM((mine * f_pad, d_model), BF16),
            pltpu.VMEM((rows, d_model), F32),
            pltpu.VMEM((n_tp - 1, 8, d_model), F32),
            pltpu.VMEM((n_dp * n_tp, 8, d_model), BF16),
            pltpu.VMEM((n_dp * n_tp * 8, d_model), BF16),
            pltpu.VMEM((n_dp * n_tp, 8, 128), F32),
            pltpu.VMEM((n_dp * n_tp * 8, mine * f_pad), BF16),
            pltpu.VMEM((chunks, 2, n_chip * 8, cw), F32),
            pltpu.VMEM((chunks, n_chip * 8, cw), F32),
            pltpu.VMEM((chunks, n_chip * 8, cw), F32),
            pltpu.VMEM((chunks, n_chip - 1, 8, cw), F32),
            pltpu.VMEM((n_tp, 8, d_model), BF16),
            dma((ring,)), dma((ring,)), dma((mine,)),
            dma((n_tp - 1,)), dma((n_tp - 1,)),
            dma((n_chip - 1,)), dma((n_chip - 1,)),
            dma((n_chip,)), dma((n_chip,)),
            dma((n_chip - 1,)), dma((n_chip - 1,)),
            dma((n_chip,)), dma((n_chip,)),
            dma((chunks,)), dma((chunks,)),
            dma((chunks, n_chip - 1)), dma((chunks, n_chip - 1)),
            dma((n_tp - 1,)), dma((n_tp - 1,)),
        ],
        compiler_params=pltpu.CompilerParams(
            collective_id=0, has_side_effects=True, vmem_limit_bytes=63 << 20),
        cost_estimate=pl.CostEstimate(flops=8_000_000_000, bytes_accessed=66_000_000, transcendentals=0),
    )(part, x, g[None, :], picks, wr, wg, wu, wd)
    return out.reshape(rows, d_model)


def solution(mesh):
    cache_spec = P("dp", None, "tp", None)
    in_specs = (P("dp", None), cache_spec, cache_spec, P("dp"), P("dp", None), P(None), P(None, "tp"), P(None, "tp"), P(None, "tp"), P("tp", None), P(None), P(None, None), P(None, None, "tp"), P(None, None, "tp"), P(None, "tp", None))
    out_specs = (P("dp", None), cache_spec, cache_spec)
    n_dp, n_tp = mesh.shape["dp"], mesh.shape["tp"]

    def layer_shard(hidden_in, k_cache, v_cache, seq_lens, chosen_experts, g_attn, w_q, w_k, w_v, w_o, g_moe, w_router, w_gate, w_up, w_down):
        rows, slots, heads, dim = k_cache.shape
        flat = (rows, slots * heads, dim)
        part, k_next, v_next = attention(
            hidden_in, k_cache.reshape(flat), v_cache.reshape(flat), seq_lens, g_attn, w_q, w_k, w_v, w_o)
        out = experts(part, hidden_in, chosen_experts.T, g_moe, w_router.T, w_gate.swapaxes(1, 2),
                      w_up.swapaxes(1, 2), w_down, n_dp, n_tp)
        return out, k_next.reshape(k_cache.shape), v_next.reshape(v_cache.shape)

    return jax.shard_map(layer_shard, mesh=mesh, in_specs=in_specs, out_specs=out_specs, check_vma=False)
```

time: 213 us -> 71.2 us (0.33)
  matrix products: 115 us -> 0 us
  Pallas kernels: 0 us -> 65.6 us
  waiting for transfers between devices: 59.7 us -> 0 us
  other arithmetic: 20.9 us -> 0.62 us
  between operations: 14.2 us -> 0.65 us
  local copies, waits for them, and re-layouts: 1.33 us -> 4.14 us
    dot_general x10 -> x0, matrix products: 115 us -> none  [the longest x1 35 us: experts_part(): jnp.einsum('bd,edf->bef', h_moe, w_up, preferred_element_type=jnp.float32)]
    pallas_call x0 -> x2, Pallas kernels: none -> 65.6 us  [the longest x1 48.4 us: experts(): pl.pallas_call(functools.partial(experts_kernel, n_dp=n_dp, n_tp=n_tp, ri...]
    psum x2 -> x0, waiting for transfers between devices: 59.7 us -> none  [the longest x1 31.2 us: layer_shard(): attn_sum = lax.psum(attn_local, 'tp')]
    select_n x1 -> x0, other arithmetic: 13.7 us -> none  [attention_part(): k_next = jnp.where(new_slot, k_new[:, None, :, :], k_cache)]
    convert_element_type x5 -> x0, other arithmetic: 3.16 us -> none  [the longest x1 1.63 us: layer_shard(): hidden_out = (hidden_mid.astype(jnp.float32) + moe_sum).astype(jnp.bfloat16)]
    broadcast_in_dim x0 -> x2, local copies, waits for them, and re-layouts: none -> 2.57 us  [the longest x1 1.29 us: attention(): g[None, :]]
    reduce_sum x5 -> x0, other arithmetic: 2.46 us -> none  [the longest x2 2.13 us: rms_norm(): jnp.mean(vector32 * vector32, axis=-1, keepdims=True) + EPSILON]
  transfers between devices with their start and end apart: 2 -> 0, of which waited for: 2 -> 0; matrix products, arithmetic and copies ran while one was open for 0% -> 0% of each run, Pallas kernels for 0% -> 0%
where the time goes in v1:
time: 71.2 us; the launch traced here: 71 us
  Pallas kernels  65.6 us (92%)
  local copies, waits for them, and re-layouts  4.14 us (6%)
    pallas_call x1, Pallas kernels, experts(): pl.pallas_call(functools.partial(experts_kernel, n_dp=n_dp, n_tp=n_tp, ri...  48.4 us
    pallas_call x1, Pallas kernels, attention(): pl.pallas_call(functools.partial(attention_kernel, group=group), name='at...  17.2 us
    unnamed x1, local copies, waits for them, and re-layouts  1.57 us

profile of v1, /device:TPU:0, one launch (start us, length us, event | category | flops | bytes accessed | tf_op | source)
XLA Modules:
  0.0 71.0 jit_solution(17670997997957233465)
XLA Ops:
  0.6 0.6 maximum_bitcast_fusion.freq_ref
  1.3 1.3 %broadcast_in_dim.9.g_ref = bf16[1,2048]{1,0:T(2,128)(2,1)} reshape(bf16[2048]{0:T(1024)(128)(2,1)} %param.20) | data formatting | bytes 8192 | tf_op jit(solution)/shard_map/broadcast_in_dim | solution.py:166
  2.5 1.3 %broadcast_in_dim.11.g_ref = bf16[1,2048]{1,0:T(2,128)(2,1)} reshape(bf16[2048]{0:T(1024)(128)(2,1)} %param.25) | data formatting | bytes 8192 | tf_op jit(solution)/shard_map/broadcast_in_dim | solution.py:433
  3.8 17.2 %attention.1 = (f32[32,2048]{1,0:T(8,128)}, bf16[32,1024,128]{2,1,0:T(8,128)(2,1)}, bf16[32,1024,128]{2,1,0:T(8,128)(2,1)}) custom-call(s32[32]{0:T(128)} %lens.1, bf16[32,2048]{1,0:T(8,128)(2,1)} %x_ref.3, bf16[1,2048]{1,0:T(2,128)(2,1)} %broadcast_in_dim.9.g_ref, f32[1,128]{1,0:T(1,128)} %maximum_bitcast_fusion.freq_ref, bf16[2048,512]{1,0:T(8,128)(2,1)} %wq.1, ...), custom_call_target="tpu_custom_call" | custom-call | flops 400000000 | bytes 42000000 | tf_op jit(solution)/shard_map/attention/pallas_call | solution.py:144
  21.0 48.4 %experts.1 = bf16[4,8,2048]{2,1,0:T(8,128)(2,1)} custom-call(f32[32,2048]{1,0:T(8,128)} %get-tuple-element.6.part, bf16[32,2048]{1,0:T(8,128)(2,1)} %x_ref.3, bf16[1,2048]{1,0:T(2,128)(2,1)} %broadcast_in_dim.11.g_ref, s32[4,32]{1,0:T(4,128)} %bitcast.15, bf16[60,2048]{1,0:T(8,128)(2,1)} %bitcast.14, bf16[60,352,2048]{2,1,0:T(8,128)(2,1)} %bitcast.5.wg, ...), custom_call_target="tpu_custom_call" | custom-call | flops 8000000000 | bytes 66000000 | tf_op jit(solution)/shard_map/experts/pallas_call | solution.py:399
  69.4 1.6 %copy.19 = bf16[32,2048]{1,0:T(8,128)(2,1)} copy(bf16[32,2048]{1,0:T(8,128)(2,1)} %bitcast.13) | data formatting | bytes 262144
  (1 shorter events, 0.0 us)

commit v2 on v1

--- a/solution.py
+++ b/solution.py
@@ -1,4 +1,5 @@
 import functools
+import math
 import jax
 import jax.numpy as jnp
 from jax import lax
@@ -20,17 +21,27 @@
 
 def norm_rows(x32, gain):
     scale = lax.rsqrt(jnp.mean(x32 * x32, axis=-1, keepdims=True) + EPSILON)
-    return (x32 * scale * gain.astype(F32)).astype(BF16)
-
-
-def attention_kernel(lens, x_ref, g_ref, freq_ref, wq, wk, wv, wo, kc, vc, part_ref, kout, vout,
-                     kbuf, vbuf, qkvw, wobuf, qs, ks, vs, os_, wsem, insem, outsem, *, group):
+    return (x32 * scale * gain).astype(BF16)
+
+
+def gain_row(g_ref):
+    g32 = g_ref[...].astype(F32)
+    return jnp.concatenate([g32[i:i + 1, :] for i in range(g32.shape[0])], axis=1)
+
+
+def attention_kernel(lens, x_hbm, g_ref, wq, wk, wv, wo, kc, vc, part_ref, kout, vout,
+                     kbuf, vbuf, x_ref, qkvw, wobuf, qs, ks, vs, os_, wsem, insem, outsem, *, group):
     rows = x_ref.shape[0]
+    width = wq.shape[1]
     heads = wq.shape[1] // 128
     slots = kc.shape[1]
     steps = rows // group
-    wcopies = [pltpu.make_async_copy(w, qkvw.at[i], wsem.at[i]) for i, w in enumerate((wq, wk, wv))]
+    half = steps // 2
+    xcopy = pltpu.make_async_copy(x_hbm, x_ref, wsem.at[4])
+    wcopies = [pltpu.make_async_copy(w, qkvw.at[:, pl.ds(i * width, width)], wsem.at[i])
+               for i, w in enumerate((wq, wk, wv))]
     wocopy = pltpu.make_async_copy(wo, wobuf, wsem.at[3])
+    xcopy.start()
     for cp in wcopies:
         cp.start()
 
@@ -42,31 +53,34 @@
         at = pl.ds(i * group, group)
         return pltpu.make_async_copy(buf.at[at], hbm.at[at], outsem.at[j, i])
 
-    for i in range(steps):
-        fetch(i, kc, kbuf, 0).start()
-        fetch(i, vc, vbuf, 1).start()
-    wocopy.start()
-
-    h = norm_rows(x_ref[...].astype(F32), g_ref[...])
+    def fetch_groups(lo, hi):
+        for i in range(lo, hi):
+            fetch(i, kc, kbuf, 0).start()
+            fetch(i, vc, vbuf, 1).start()
+
     row_id = lax.broadcasted_iota(jnp.int32, (rows, 128), 0)
     pos = jnp.zeros((rows, 128), jnp.int32)
     for b in range(rows):
         pos = jnp.where(row_id == b, lens[b], pos)
-    ang = pos.astype(F32) * freq_ref[...]
+    lane = lax.broadcasted_iota(jnp.int32, (rows, 128), 1)
+    freq = jnp.exp(lax.rem(lane, 64).astype(F32) * (-2.0 * math.log(ROPE_THETA) / 128))
+    ang = pos.astype(F32) * freq
     cos_t = jnp.cos(ang)
     sin_t = jnp.sin(ang)
-    lane = lax.broadcasted_iota(jnp.int32, (rows, 128), 1)
     sin_t = jnp.where(lane < 64, -sin_t, sin_t)
 
     def rope(u):
         return u * cos_t + pltpu.roll(u, 64, 1) * sin_t
 
-    wcopies[0].wait()
-    q = jnp.dot(h, qkvw[0], preferred_element_type=F32)
-    wcopies[1].wait()
-    k = jnp.dot(h, qkvw[1], preferred_element_type=F32)
-    wcopies[2].wait()
-    v = jnp.dot(h, qkvw[2], preferred_element_type=F32)
+    xcopy.wait()
+    h = norm_rows(x_ref[...].astype(F32), gain_row(g_ref))
+    fetch_groups(0, 1)
+    for cp in wcopies:
+        cp.wait()
+    fetch_groups(1, half)
+    qkv = jnp.dot(h, qkvw[...], preferred_element_type=F32)
+    q, k, v = (qkv[:, i * width:(i + 1) * width] for i in range(3))
+    fetch_groups(half, half + 2)
     for j in range(heads):
         cols = slice(128 * j, 128 * j + 128)
         qs[pl.ds(j, rows, stride=heads), :] = rope(q[:, cols]).astype(BF16).astype(F32)
@@ -98,7 +112,15 @@
         ps = [lens[i * group + u] for u in range(group)]
         for u in range(group):
             insert(kbuf, ks, i * group + u, ps[u])
-        flush(i, kout, kbuf, 0).start()
+        @pl.when(i == 0)
+        def _():
+            fetch_groups(half + 2, steps)
+            wocopy.start()
+
+        @pl.when(i >= half)
+        def _():
+            flush(i, kout, kbuf, 0).start()
+
         sc = jnp.zeros((qrows, slots), F32)
         pm = jnp.zeros((qrows, slots), jnp.int32)
         for u in range(group):
@@ -111,7 +133,17 @@
         fetch(i, vc, vbuf, 1).wait()
         for u in range(group):
             insert(vbuf, vs, i * group + u, ps[u])
-        flush(i, vout, vbuf, 1).start()
+
+        @pl.when(i >= half)
+        def _():
+            flush(i, vout, vbuf, 1).start()
+
+        @pl.when(i == half - 1)
+        def _():
+            for u in range(half):
+                flush(u, kout, kbuf, 0).start()
+                flush(u, vout, vbuf, 1).start()
+
         o = jnp.zeros((qrows, 128), F32)
         for u in range(group):
             o_u = jnp.dot(wt, vbuf[i * group + u], preferred_element_type=F32)
@@ -139,45 +171,45 @@
     heads = width // 128
     group = 4
     steps = rows // group
-    freq = ROPE_THETA ** (-jnp.arange(0, 128, 2, dtype=F32) / 128)
-    freq = jnp.concatenate([freq, freq])[None, :]
     return pl.pallas_call(
         functools.partial(attention_kernel, group=group),
         name="attention",
         out_shape=(jax.ShapeDtypeStruct((rows, d_model), F32),
                    jax.ShapeDtypeStruct(kc.shape, BF16), jax.ShapeDtypeStruct(vc.shape, BF16)),
-        in_specs=[SMEM, VMEM, VMEM, VMEM, ANY, ANY, ANY, ANY, ANY, ANY],
+        in_specs=[SMEM, ANY, VMEM, ANY, ANY, ANY, ANY, ANY, ANY],
         out_specs=(VMEM, ANY, ANY),
         scratch_shapes=[
             pltpu.VMEM((rows, slots, 128), BF16),
             pltpu.VMEM((rows, slots, 128), BF16),
-            pltpu.VMEM((3, d_model, width), BF16),
+            pltpu.VMEM((rows, d_model), BF16),
+            pltpu.VMEM((d_model, 3 * width), BF16),
             pltpu.VMEM((width, d_model), BF16),
             pltpu.VMEM((rows * heads, 128), F32),
             pltpu.VMEM((rows * 8, 128), F32),
             pltpu.VMEM((rows * 8, 128), F32),
             pltpu.VMEM((rows * heads, 128), F32),
-            pltpu.SemaphoreType.DMA((4,)),
+            pltpu.SemaphoreType.DMA((5,)),
             pltpu.SemaphoreType.DMA((2, steps)),
             pltpu.SemaphoreType.DMA((2, steps)),
         ],
         compiler_params=pltpu.CompilerParams(vmem_limit_bytes=63 << 20),
         cost_estimate=pl.CostEstimate(flops=400_000_000, bytes_accessed=42_000_000, transcendentals=0),
-    )(lens, x, g[None, :], freq, wq, wk, wv, wo, kc, vc)
-
-
-def experts_kernel(part, x_ref, g_ref, picks, wr, wg, wu, wd, out_ref,
-                   gbuf, ubuf, dbuf, xf, recv1, hall, hb, gall, z, acc, drecv, psum, frecv, yall,
+    )(lens, x, g.reshape(-1, 128), wq, wk, wv, wo, kc, vc)
+
+
+def experts_kernel(part_hbm, x_hbm, g_ref, picks, wr_hbm, wg, wu, wd, out_hbm,
+                   part, x_ref, wr, lsem, osem, gbuf, ubuf, dbuf, xf, recv1, hall, hb, gall, z, acc, drecv, psum, frecv, yall,
                    gsem, usem, dsem, s1, r1, s2, r2, s3, r3, s4, r4, s5, r5, s6, r6, s7, r7, s8, r8,
-                   *, n_dp, n_tp, ring, chunks):
+                   *, n_dp, n_tp, n_exp, ring, batch, chunks):
     dp = lax.axis_index("dp")
     tp = lax.axis_index("tp")
     core = lax.rem(tp, 2)
     xx = lax.div(tp, 2)
-    n_exp, f_dim, d_model = wg.shape
+    d_model = wg.shape[1]
+    f_dim = wg.shape[0] // n_exp
     mine = n_exp // n_dp
     base = dp * mine
-    f_pad = z.shape[1] // mine
+    batches = [(e, min(batch, mine - e)) for e in range(0, mine, batch)]
     n_chip = n_dp * n_tp // 2
     me_chip = dp * (n_tp // 2) + xx
     me = dp * n_tp + tp
@@ -200,23 +232,32 @@
     partner = {"dp": dp, "tp": 2 * xx + 1 - core}
     cross = {"dp": dp, "tp": 2 * (1 - xx) + 1 - core}
 
-    def gcopy(e, s):
-        return pltpu.make_async_copy(wg.at[base + e], gbuf.at[s], gsem.at[s])
-
-    def ucopy(e, s):
-        return pltpu.make_async_copy(wu.at[base + e], ubuf.at[s], usem.at[s])
-
-    def dcopy(e):
-        return pltpu.make_async_copy(wd.at[base + e], dbuf.at[pl.ds(e * f_pad, f_dim)], dsem.at[e])
+    def weights(b):
+        e, n = batches[b]
+        src = pl.ds(pl.multiple_of((base + e) * f_dim, f_dim), n * f_dim)
+        s = b % ring
+        return (pltpu.make_async_copy(wg.at[src], gbuf.at[s, pl.ds(0, n * f_dim)], gsem.at[s]),
+                pltpu.make_async_copy(wu.at[src], ubuf.at[s, pl.ds(0, n * f_dim)], usem.at[s]))
+
+    def down_weights(b):
+        e, n = batches[b]
+        src = pl.ds(pl.multiple_of((base + e) * f_dim, f_dim), n * f_dim)
+        return pltpu.make_async_copy(wd.at[src], dbuf.at[pl.ds(e * f_dim, n * f_dim)], dsem.at[b])
+
+    def start(b):
+        for cp in weights(b):
+            cp.start()
 
     barrier = pltpu.get_barrier_semaphore()
     for dev in peers + [partner, cross]:
         pl.semaphore_signal(barrier, inc=1, device_id=dev, device_id_type=MESH)
-    for e in range(ring):
-        gcopy(e, e).start()
-        ucopy(e, e).start()
-    for e in range(mine):
-        dcopy(e).start()
+    loads = [pltpu.make_async_copy(a, b, lsem.at[i])
+             for i, (a, b) in enumerate(((part_hbm, part), (x_hbm, x_ref), (wr_hbm, wr)))]
+    for cp in loads:
+        cp.start()
+    start(0)
+    for cp in loads:
+        cp.wait()
     xf[...] = x_ref[...].astype(F32)
     pl.semaphore_wait(barrier, len(peers) + 2)
 
@@ -233,9 +274,7 @@
         cp.start()
         first.append(cp)
 
-    for e in range(mine):
-        dbuf[pl.ds(e * f_pad + f_dim, f_pad - f_dim), :] = jnp.zeros((f_pad - f_dim, d_model), BF16)
-    z[...] = jnp.zeros_like(z)
+    start(1)
     pick_cols = []
     row8 = lax.broadcasted_iota(jnp.int32, (8, 128), 0)
     for kk in range(picks.shape[0]):
@@ -251,7 +290,7 @@
         attn_sum = attn_sum + recv1[k - 1]
     x1 = (xf[block(tp), :] + attn_sum).astype(BF16).astype(F32)
     xf[block(tp), :] = x1
-    h2 = norm_rows(x1, g_ref[...])
+    h2 = norm_rows(x1, gain_row(g_ref))
     hall[me] = h2
 
     def spread(buf, i, m, ssem, rsem):
@@ -270,6 +309,7 @@
     for m in order:
         hs[m].start()
     hd[0].start()
+    start(2)
 
     logits = lax.dot_general(h2, wr[...], NT, preferred_element_type=F32)
     lane = lax.broadcasted_iota(jnp.int32, (8, 128), 1)
@@ -315,27 +355,43 @@
     gmat = gall[...].reshape(n_blk * 8, 128)
     glane = lax.broadcasted_iota(jnp.int32, (n_blk * 8, 128), 1)
 
-    def expert(e, s):
-        gcopy(e, s).wait()
-        ucopy(e, s).wait()
-        gate = lax.dot_general(hb[...], gbuf[s], NT, preferred_element_type=F32)
-        up = lax.dot_general(hb[...], ubuf[s], NT, preferred_element_type=F32)
-        gcol = jnp.sum(jnp.where(glane == base + e, gmat, 0.0), axis=1, keepdims=True)
-        return (gcol * (gate * jax.nn.sigmoid(gate)) * up).astype(BF16)
-
-    unroll = 3
-    for e0 in range(0, mine, unroll):
-        for e in range(e0, e0 + unroll):
-            s = e % ring
-            z[:, e * f_pad:e * f_pad + f_dim] = expert(e, s)
-            if e + ring < mine:
-                gcopy(e + ring, s).start()
-                ucopy(e + ring, s).start()
-
-    for e in range(mine):
-        dcopy(e).wait()
-
-    pend = []
+    def products(b):
+        s, width = b % ring, batches[b][1] * f_dim
+        for cp in weights(b):
+            cp.wait()
+        gate = lax.dot_general(hb[...], gbuf[s, :width], NT, preferred_element_type=F32)
+        up = lax.dot_general(hb[...], ubuf[s, :width], NT, preferred_element_type=F32)
+        if b + ring < len(batches):
+            start(b + ring)
+        return gate, up
+
+    def activate(b, gate, up):
+        e0, n = batches[b]
+        cols = [jnp.sum(jnp.where(glane == base + e, gmat, 0.0), axis=1, keepdims=True)
+                for e in range(e0, e0 + n)]
+        for lo in range(0, n * f_dim, 128):
+            hi = min(lo + 128, n * f_dim)
+            ea, eb = lo // f_dim, (hi - 1) // f_dim
+            gcol = cols[ea]
+            if eb > ea:
+                gcol = jnp.where(glane[:, :hi - lo] < eb * f_dim - lo, cols[ea], cols[eb])
+            ga = gate[:, lo:hi]
+            at = e0 * f_dim + lo
+            z[:, at:at + hi - lo] = (gcol * (ga * jax.nn.sigmoid(ga)) * up[:, lo:hi]).astype(BF16)
+
+    for b in range(len(batches)):
+        down_weights(b).start()
+    before = None
+    for b in range(len(batches)):
+        now = products(b)
+        if before is not None:
+            activate(b - 1, *before)
+        before = now
+    activate(len(batches) - 1, *before)
+    for b in range(len(batches)):
+        down_weights(b).wait()
+
+    lag = 1
     finals = {}
     pair = {}
 
@@ -362,9 +418,11 @@
             device_id=partner, device_id_type=MESH)
         cp.start()
         pair[n] = cp
-        if n >= 1:
-            pair_sum(n - 1)
-    pair_sum(chunks - 1)
+        if n >= lag:
+            pair_sum(n - lag)
+    for n in range(chunks - lag, chunks):
+        pair_sum(n)
+    last = []
     for n in range(chunks):
         total = psum[n, block(me_chip), :]
         for m in range(n_chip - 1):
@@ -372,17 +430,26 @@
             total = total + frecv[n, m]
         cols = slice(n * cw, (n + 1) * cw)
         yall[tp, :, cols] = (xf[block(tp), cols] + total).astype(BF16)
-    last = []
-    for k in range(1, n_tp):
-        t_to = lax.rem(tp + k, n_tp)
-        cp = pltpu.make_async_remote_copy(
-            src_ref=yall.at[tp], dst_ref=yall.at[tp], send_sem=s8.at[k - 1], recv_sem=r8.at[k - 1],
-            device_id={"dp": dp, "tp": t_to}, device_id_type=MESH)
-        cp.start()
-        last.append(cp)
-    for cp in last:
-        cp.wait_recv()
-    out_ref[...] = yall[...]
+        if n % 2 == 1:
+            span = pl.ds((n - 1) * cw, 2 * cw)
+            for k in range(1, n_tp):
+                t_to = lax.rem(tp + k, n_tp)
+                cp = pltpu.make_async_remote_copy(
+                    src_ref=yall.at[tp, :, span], dst_ref=yall.at[tp, :, span],
+                    send_sem=s8.at[n // 2, k - 1], recv_sem=r8.at[n // 2, k - 1],
+                    device_id={"dp": dp, "tp": t_to}, device_id_type=MESH)
+                cp.start()
+                last.append(cp)
+    outs = []
+    for n in range(chunks // 2):
+        span = pl.ds(2 * n * cw, 2 * cw)
+        for cp in last[n * (n_tp - 1):(n + 1) * (n_tp - 1)]:
+            cp.wait_recv()
+        cp = pltpu.make_async_copy(yall.at[:, :, span], out_hbm.at[:, :, span], osem.at[n])
+        cp.start()
+        outs.append(cp)
+    for cp in outs:
+        cp.wait()
     for cp in last + list(pair.values()) + list(finals.values()):
         cp.wait_send()
 
@@ -391,33 +458,39 @@
     rows, d_model = x.shape
     n_exp, f_dim, _ = wg.shape
     mine = n_exp // n_dp
-    f_pad = -(-f_dim // 128) * 128
-    ring, chunks = 10, 4
+    ring, batch, chunks = 3, 4, 4
+    n_batch = -(-mine // batch)
+    wg, wu, wd = (w.reshape(n_exp * f_dim, d_model) for w in (wg, wu, wd))
     n_chip = n_dp * n_tp // 2
     cw = d_model // chunks
     dma = pltpu.SemaphoreType.DMA
     out = pl.pallas_call(
-        functools.partial(experts_kernel, n_dp=n_dp, n_tp=n_tp, ring=ring, chunks=chunks),
+        functools.partial(experts_kernel, n_dp=n_dp, n_tp=n_tp, n_exp=n_exp, ring=ring, batch=batch,
+                          chunks=chunks),
         name="experts",
         out_shape=jax.ShapeDtypeStruct((n_tp, 8, d_model), BF16),
-        in_specs=[VMEM, VMEM, VMEM, SMEM, VMEM, ANY, ANY, ANY],
-        out_specs=VMEM,
+        in_specs=[ANY, ANY, VMEM, SMEM, ANY, ANY, ANY, ANY],
+        out_specs=ANY,
         scratch_shapes=[
-            pltpu.VMEM((ring, f_dim, d_model), BF16),
-            pltpu.VMEM((ring, f_dim, d_model), BF16),
-            pltpu.VMEM((mine * f_pad, d_model), BF16),
+            pltpu.VMEM((rows, d_model), F32),
+            pltpu.VMEM((rows, d_model), BF16),
+            pltpu.VMEM(wr.shape, BF16),
+            dma((3,)), dma((chunks // 2,)),
+            pltpu.VMEM((ring, batch * f_dim, d_model), BF16),
+            pltpu.VMEM((ring, batch * f_dim, d_model), BF16),
+            pltpu.VMEM((mine * f_dim, d_model), BF16),
             pltpu.VMEM((rows, d_model), F32),
             pltpu.VMEM((n_tp - 1, 8, d_model), F32),
             pltpu.VMEM((n_dp * n_tp, 8, d_model), BF16),
             pltpu.VMEM((n_dp * n_tp * 8, d_model), BF16),
             pltpu.VMEM((n_dp * n_tp, 8, 128), F32),
-            pltpu.VMEM((n_dp * n_tp * 8, mine * f_pad), BF16),
+            pltpu.VMEM((n_dp * n_tp * 8, mine * f_dim), BF16),
             pltpu.VMEM((chunks, 2, n_chip * 8, cw), F32),
             pltpu.VMEM((chunks, n_chip * 8, cw), F32),
             pltpu.VMEM((chunks, n_chip * 8, cw), F32),
             pltpu.VMEM((chunks, n_chip - 1, 8, cw), F32),
             pltpu.VMEM((n_tp, 8, d_model), BF16),
-            dma((ring,)), dma((ring,)), dma((mine,)),
+            dma((ring,)), dma((ring,)), dma((n_batch,)),
             dma((n_tp - 1,)), dma((n_tp - 1,)),
             dma((n_chip - 1,)), dma((n_chip - 1,)),
             dma((n_chip,)), dma((n_chip,)),
@@ -425,12 +498,12 @@
             dma((n_chip,)), dma((n_chip,)),
             dma((chunks,)), dma((chunks,)),
             dma((chunks, n_chip - 1)), dma((chunks, n_chip - 1)),
-            dma((n_tp - 1,)), dma((n_tp - 1,)),
+            dma((chunks // 2, n_tp - 1)), dma((chunks // 2, n_tp - 1)),
         ],
         compiler_params=pltpu.CompilerParams(
             collective_id=0, has_side_effects=True, vmem_limit_bytes=63 << 20),
         cost_estimate=pl.CostEstimate(flops=8_000_000_000, bytes_accessed=66_000_000, transcendentals=0),
-    )(part, x, g[None, :], picks, wr, wg, wu, wd)
+    )(part, x, g.reshape(-1, 128), picks, wr, wg, wu, wd)
     return out.reshape(rows, d_model)
 
 

time: 71.2 us -> 64.4 us (0.904)
  Pallas kernels: 65.6 us -> 62 us
  local copies, waits for them, and re-layouts: 4.14 us -> 1.57 us
    broadcast_in_dim x2 -> x0, local copies, waits for them, and re-layouts: 2.57 us -> none  [the longest x1 1.29 us: attention(): g[None, :]]
    pallas_call x1, Pallas kernels: 48.4 us -> 46.2 us  [experts(): pl.pallas_call(functools.partial(experts_kernel, n_dp=n_dp, n_tp=n_tp, n_...]
    pallas_call x1, Pallas kernels: 17.2 us -> 15.8 us  [attention(): pl.pallas_call(functools.partial(attention_kernel, group=group), name='at...]
where the time goes in v2:
time: 64.4 us; the launch traced here: 64.2 us
  Pallas kernels  62 us (96%)
  local copies, waits for them, and re-layouts  1.57 us (2%)
  between operations  0.65 us (1%)
    pallas_call x1, Pallas kernels, experts(): pl.pallas_call(functools.partial(experts_kernel, n_dp=n_dp, n_tp=n_tp, n_...  46.2 us
    pallas_call x1, Pallas kernels, attention(): pl.pallas_call(functools.partial(attention_kernel, group=group), name='at...  15.8 us
    unnamed x1, local copies, waits for them, and re-layouts  1.57 us

profile of v2, /device:TPU:0, one launch (start us, length us, event | category | flops | bytes accessed | tf_op | source)
XLA Modules:
  0.0 64.2 jit_solution(12775594589145649086)
XLA Ops:
  0.6 15.8 %attention.1 = (f32[32,2048]{1,0:T(8,128)}, bf16[32,1024,128]{2,1,0:T(8,128)(2,1)}, bf16[32,1024,128]{2,1,0:T(8,128)(2,1)}) custom-call(s32[32]{0:T(128)} %lens.1, bf16[32,2048]{1,0:T(8,128)(2,1)} %x_hbm.3, bf16[16,128]{1,0:T(8,128)(2,1)} %bitcast.20, bf16[2048,512]{1,0:T(8,128)(2,1)} %wq.1, bf16[2048,512]{1,0:T(8,128)(2,1)} %wk.1, bf16[2048,512]{1,0:T(8,128)(2,1)} %wv.1, ...), custom_call_target="tpu_custom_call" | custom-call | flops 400000000 | bytes 42000000 | tf_op jit(solution)/shard_map/attention/pallas_call | solution.py:174
  16.5 46.2 %experts.1 = bf16[4,8,2048]{2,1,0:T(8,128)(2,1)} custom-call(f32[32,2048]{1,0:T(8,128)} %get-tuple-element.6.part_hbm, bf16[32,2048]{1,0:T(8,128)(2,1)} %x_hbm.3, bf16[16,128]{1,0:T(8,128)(2,1)} %bitcast.21, s32[4,32]{1,0:T(4,128)} %bitcast.22, bf16[60,2048]{1,0:T(8,128)(2,1)} %bitcast.19, bf16[21120,2048]{1,0:T(8,128)(2,1)} %bitcast.7.wg, ...), custom_call_target="tpu_custom_call" | custom-call | flops 8000000000 | bytes 66000000 | tf_op jit(solution)/shard_map/experts/pallas_call | solution.py:467
  62.7 1.6 %copy.19 = bf16[32,2048]{1,0:T(8,128)(2,1)} copy(bf16[32,2048]{1,0:T(8,128)(2,1)} %bitcast.18) | data formatting | bytes 262144

commit v3 on v2

--- a/solution.py
+++ b/solution.py
@@ -198,7 +198,7 @@
 
 
 def experts_kernel(part_hbm, x_hbm, g_ref, picks, wr_hbm, wg, wu, wd, out_hbm,
-                   part, x_ref, wr, lsem, osem, gbuf, ubuf, dbuf, xf, recv1, hall, hb, gall, z, acc, drecv, psum, frecv, yall,
+                   part, x_ref, wr, lsem, osem, gbuf, ubuf, dbuf, xf, recv1, hall, hb, gall, gt, z, acc, drecv, psum, frecv, yall,
                    gsem, usem, dsem, s1, r1, s2, r2, s3, r3, s4, r4, s5, r5, s6, r6, s7, r7, s8, r8,
                    *, n_dp, n_tp, n_exp, ring, batch, chunks):
     dp = lax.axis_index("dp")
@@ -255,9 +255,9 @@
              for i, (a, b) in enumerate(((part_hbm, part), (x_hbm, x_ref), (wr_hbm, wr)))]
     for cp in loads:
         cp.start()
-    start(0)
     for cp in loads:
         cp.wait()
+    start(0)
     xf[...] = x_ref[...].astype(F32)
     pl.semaphore_wait(barrier, len(peers) + 2)
 
@@ -339,51 +339,52 @@
         cp = relay(hall, owner(m), m, s3, r3)
         cp.start()
         hd.append(cp)
-    for m in reversed(order):
-        gs[m].wait_recv()
-        cp = relay(gall, owner(m), m, s5, r5)
-        cp.start()
-        gd.append(cp)
-    for cp in hd + gd:
+    for cp in hd:
         cp.wait_recv()
-    for cp in hs + gs + hd + gd:
-        cp.wait_send()
 
     for r in range(n_blk // 2):
         two = jnp.concatenate([hall[2 * r].astype(F32), hall[2 * r + 1].astype(F32)], axis=0)
         hb[16 * r:16 * r + 16, :] = two.astype(BF16)
-    gmat = gall[...].reshape(n_blk * 8, 128)
-    glane = lax.broadcasted_iota(jnp.int32, (n_blk * 8, 128), 1)
-
     def products(b):
         s, width = b % ring, batches[b][1] * f_dim
         for cp in weights(b):
             cp.wait()
-        gate = lax.dot_general(hb[...], gbuf[s, :width], NT, preferred_element_type=F32)
-        up = lax.dot_general(hb[...], ubuf[s, :width], NT, preferred_element_type=F32)
+        gate = lax.dot_general(gbuf[s, :width], hb[...], NT, preferred_element_type=F32)
+        up = lax.dot_general(ubuf[s, :width], hb[...], NT, preferred_element_type=F32)
         if b + ring < len(batches):
             start(b + ring)
         return gate, up
 
     def activate(b, gate, up):
         e0, n = batches[b]
-        cols = [jnp.sum(jnp.where(glane == base + e, gmat, 0.0), axis=1, keepdims=True)
-                for e in range(e0, e0 + n)]
+        brow = lax.broadcasted_iota(jnp.int32, (128, n_blk * 8), 0)
+        rows_g = [gt[pl.ds(base + e, 1), :] for e in range(e0, e0 + n)]
         for lo in range(0, n * f_dim, 128):
             hi = min(lo + 128, n * f_dim)
             ea, eb = lo // f_dim, (hi - 1) // f_dim
-            gcol = cols[ea]
+            grow = rows_g[ea]
             if eb > ea:
-                gcol = jnp.where(glane[:, :hi - lo] < eb * f_dim - lo, cols[ea], cols[eb])
-            ga = gate[:, lo:hi]
+                grow = jnp.where(brow[:hi - lo] < eb * f_dim - lo, rows_g[ea], rows_g[eb])
+            ga = gate[lo:hi]
             at = e0 * f_dim + lo
-            z[:, at:at + hi - lo] = (gcol * (ga * jax.nn.sigmoid(ga)) * up[:, lo:hi]).astype(BF16)
+            zt = (grow * (ga * jax.nn.sigmoid(ga)) * up[lo:hi]).astype(BF16)
+            z[:, at:at + hi - lo] = zt.T
 
     for b in range(len(batches)):
         down_weights(b).start()
     before = None
     for b in range(len(batches)):
         now = products(b)
+        if b == 0:
+            for m in reversed(order):
+                gs[m].wait_recv()
+                cp = relay(gall, owner(m), m, s5, r5)
+                cp.start()
+                gd.append(cp)
+        if b == 1:
+            for cp in gd:
+                cp.wait_recv()
+            gt[...] = gall[...].reshape(n_blk * 8, 128).T
         if before is not None:
             activate(b - 1, *before)
         before = now
@@ -430,28 +431,27 @@
             total = total + frecv[n, m]
         cols = slice(n * cw, (n + 1) * cw)
         yall[tp, :, cols] = (xf[block(tp), cols] + total).astype(BF16)
-        if n % 2 == 1:
-            span = pl.ds((n - 1) * cw, 2 * cw)
-            for k in range(1, n_tp):
-                t_to = lax.rem(tp + k, n_tp)
-                cp = pltpu.make_async_remote_copy(
-                    src_ref=yall.at[tp, :, span], dst_ref=yall.at[tp, :, span],
-                    send_sem=s8.at[n // 2, k - 1], recv_sem=r8.at[n // 2, k - 1],
-                    device_id={"dp": dp, "tp": t_to}, device_id_type=MESH)
-                cp.start()
-                last.append(cp)
+        span = pl.ds(n * cw, cw)
+        for k in (2, 1, 3):
+            t_to = lax.rem(tp + k, n_tp)
+            cp = pltpu.make_async_remote_copy(
+                src_ref=yall.at[tp, :, span], dst_ref=yall.at[tp, :, span],
+                send_sem=s8.at[n, k - 1], recv_sem=r8.at[n, k - 1],
+                device_id={"dp": dp, "tp": t_to}, device_id_type=MESH)
+            cp.start()
+            last.append(cp)
     outs = []
-    for n in range(chunks // 2):
-        span = pl.ds(2 * n * cw, 2 * cw)
+    for n in range(chunks):
+        span = pl.ds(n * cw, cw)
         for cp in last[n * (n_tp - 1):(n + 1) * (n_tp - 1)]:
             cp.wait_recv()
         cp = pltpu.make_async_copy(yall.at[:, :, span], out_hbm.at[:, :, span], osem.at[n])
         cp.start()
         outs.append(cp)
+    for cp in hs + gs + hd + gd + list(pair.values()) + list(finals.values()) + last:
+        cp.wait_send()
     for cp in outs:
         cp.wait()
-    for cp in last + list(pair.values()) + list(finals.values()):
-        cp.wait_send()
 
 
 def experts(part, x, picks, g, wr, wg, wu, wd, n_dp, n_tp):
@@ -475,7 +475,7 @@
             pltpu.VMEM((rows, d_model), F32),
             pltpu.VMEM((rows, d_model), BF16),
             pltpu.VMEM(wr.shape, BF16),
-            dma((3,)), dma((chunks // 2,)),
+            dma((3,)), dma((chunks,)),
             pltpu.VMEM((ring, batch * f_dim, d_model), BF16),
             pltpu.VMEM((ring, batch * f_dim, d_model), BF16),
             pltpu.VMEM((mine * f_dim, d_model), BF16),
@@ -484,6 +484,7 @@
             pltpu.VMEM((n_dp * n_tp, 8, d_model), BF16),
             pltpu.VMEM((n_dp * n_tp * 8, d_model), BF16),
             pltpu.VMEM((n_dp * n_tp, 8, 128), F32),
+            pltpu.VMEM((128, n_dp * n_tp * 8), F32),
             pltpu.VMEM((n_dp * n_tp * 8, mine * f_dim), BF16),
             pltpu.VMEM((chunks, 2, n_chip * 8, cw), F32),
             pltpu.VMEM((chunks, n_chip * 8, cw), F32),
@@ -498,7 +499,7 @@
             dma((n_chip,)), dma((n_chip,)),
             dma((chunks,)), dma((chunks,)),
             dma((chunks, n_chip - 1)), dma((chunks, n_chip - 1)),
-            dma((chunks // 2, n_tp - 1)), dma((chunks // 2, n_tp - 1)),
+            dma((chunks, n_tp - 1)), dma((chunks, n_tp - 1)),
         ],
         compiler_params=pltpu.CompilerParams(
             collective_id=0, has_side_effects=True, vmem_limit_bytes=63 << 20),

time: 64.4 us -> 61.7 us (0.958)
  Pallas kernels: 62 us -> 59.2 us
    pallas_call x1, Pallas kernels: 46.2 us -> 43.4 us  [experts(): pl.pallas_call(functools.partial(experts_kernel, n_dp=n_dp, n_tp=n_tp, n_...]
where the time goes in v3:
time: 61.7 us; the launch traced here: 61.4 us
  Pallas kernels  59.2 us (96%)
  local copies, waits for them, and re-layouts  1.57 us (3%)
  between operations  0.65 us (1%)
    pallas_call x1, Pallas kernels, experts(): pl.pallas_call(functools.partial(experts_kernel, n_dp=n_dp, n_tp=n_tp, n_...  43.4 us
    pallas_call x1, Pallas kernels, attention(): pl.pallas_call(functools.partial(attention_kernel, group=group), name='at...  15.8 us
    unnamed x1, local copies, waits for them, and re-layouts  1.57 us

profile of v3, /device:TPU:0, one launch (start us, length us, event | category | flops | bytes accessed | tf_op | source)
XLA Modules:
  0.0 61.4 jit_solution(7374492245504977543)
XLA Ops:
  0.6 15.8 %attention.1 = (f32[32,2048]{1,0:T(8,128)}, bf16[32,1024,128]{2,1,0:T(8,128)(2,1)}, bf16[32,1024,128]{2,1,0:T(8,128)(2,1)}) custom-call(s32[32]{0:T(128)} %lens.1, bf16[32,2048]{1,0:T(8,128)(2,1)} %x_hbm.3, bf16[16,128]{1,0:T(8,128)(2,1)} %bitcast.20, bf16[2048,512]{1,0:T(8,128)(2,1)} %wq.1, bf16[2048,512]{1,0:T(8,128)(2,1)} %wk.1, bf16[2048,512]{1,0:T(8,128)(2,1)} %wv.1, ...), custom_call_target="tpu_custom_call" | custom-call | flops 400000000 | bytes 42000000 | tf_op jit(solution)/shard_map/attention/pallas_call | solution.py:174
  16.5 43.4 %experts.1 = bf16[4,8,2048]{2,1,0:T(8,128)(2,1)} custom-call(f32[32,2048]{1,0:T(8,128)} %get-tuple-element.6.part_hbm, bf16[32,2048]{1,0:T(8,128)(2,1)} %x_hbm.3, bf16[16,128]{1,0:T(8,128)(2,1)} %bitcast.21, s32[4,32]{1,0:T(4,128)} %bitcast.22, bf16[60,2048]{1,0:T(8,128)(2,1)} %bitcast.19, bf16[21120,2048]{1,0:T(8,128)(2,1)} %bitcast.7.wg, ...), custom_call_target="tpu_custom_call" | custom-call | flops 8000000000 | bytes 66000000 | tf_op jit(solution)/shard_map/experts/pallas_call | solution.py:467
  59.9 1.6 %copy.19 = bf16[32,2048]{1,0:T(8,128)(2,1)} copy(bf16[32,2048]{1,0:T(8,128)(2,1)} %bitcast.18) | data formatting | bytes 262144

commit v4 on v3

--- a/solution.py
+++ b/solution.py
@@ -16,7 +16,6 @@
 NT = (((1,), (1,)), ((), ()))
 ANY = pl.BlockSpec(memory_space=pl.ANY)
 VMEM = pl.BlockSpec(memory_space=pltpu.VMEM)
-SMEM = pl.BlockSpec(memory_space=pltpu.SMEM)
 
 
 def norm_rows(x32, gain):
@@ -29,20 +28,20 @@
     return jnp.concatenate([g32[i:i + 1, :] for i in range(g32.shape[0])], axis=1)
 
 
-def attention_kernel(lens, x_hbm, g_ref, wq, wk, wv, wo, kc, vc, part_ref, kout, vout,
-                     kbuf, vbuf, x_ref, qkvw, wobuf, qs, ks, vs, os_, wsem, insem, outsem, *, group):
+def attention_kernel(lens_hbm, x_hbm, g_hbm, wq, wk, wv, wo, kc, vc, part_ref, kout, vout,
+                     kbuf, vbuf, lens, x_ref, g_ref, qkvw, wobuf, qs, ks, vs, os_, wsem, insem, outsem, *, group):
     rows = x_ref.shape[0]
     width = wq.shape[1]
     heads = wq.shape[1] // 128
     slots = kc.shape[1]
     steps = rows // group
     half = steps // 2
-    xcopy = pltpu.make_async_copy(x_hbm, x_ref, wsem.at[4])
+    small = [pltpu.make_async_copy(a, b, wsem.at[4 + i])
+             for i, (a, b) in enumerate(((lens_hbm, lens), (x_hbm, x_ref), (g_hbm, g_ref)))]
     wcopies = [pltpu.make_async_copy(w, qkvw.at[:, pl.ds(i * width, width)], wsem.at[i])
                for i, w in enumerate((wq, wk, wv))]
     wocopy = pltpu.make_async_copy(wo, wobuf, wsem.at[3])
-    xcopy.start()
-    for cp in wcopies:
+    for cp in small + wcopies:
         cp.start()
 
     def fetch(i, hbm, buf, j):
@@ -51,13 +50,14 @@
 
     def flush(i, hbm, buf, j):
         at = pl.ds(i * group, group)
-        return pltpu.make_async_copy(buf.at[at], hbm.at[at], outsem.at[j, i])
+        return pltpu.make_async_copy(buf.at[at], hbm.at[at], outsem.at[j])
 
     def fetch_groups(lo, hi):
         for i in range(lo, hi):
             fetch(i, kc, kbuf, 0).start()
             fetch(i, vc, vbuf, 1).start()
 
+    small[0].wait()
     row_id = lax.broadcasted_iota(jnp.int32, (rows, 128), 0)
     pos = jnp.zeros((rows, 128), jnp.int32)
     for b in range(rows):
@@ -72,7 +72,8 @@
     def rope(u):
         return u * cos_t + pltpu.roll(u, 64, 1) * sin_t
 
-    xcopy.wait()
+    for cp in small[1:]:
+        cp.wait()
     h = norm_rows(x_ref[...].astype(F32), gain_row(g_ref))
     fetch_groups(0, 1)
     for cp in wcopies:
@@ -156,12 +157,8 @@
     wocopy.wait()
     part_ref[...] = jnp.dot(o, wobuf[...], preferred_element_type=F32)
 
-    def drain(i, carry):
-        flush(i, kout, kbuf, 0).wait()
-        flush(i, vout, vbuf, 1).wait()
-        return carry
-
-    lax.fori_loop(0, steps, drain, 0)
+    pltpu.make_async_copy(kbuf, kout, outsem.at[0]).wait()
+    pltpu.make_async_copy(vbuf, vout, outsem.at[1]).wait()
 
 
 def attention(x, kc, vc, lens, g, wq, wk, wv, wo):
@@ -176,29 +173,31 @@
         name="attention",
         out_shape=(jax.ShapeDtypeStruct((rows, d_model), F32),
                    jax.ShapeDtypeStruct(kc.shape, BF16), jax.ShapeDtypeStruct(vc.shape, BF16)),
-        in_specs=[SMEM, ANY, VMEM, ANY, ANY, ANY, ANY, ANY, ANY],
+        in_specs=[ANY] * 9,
         out_specs=(VMEM, ANY, ANY),
         scratch_shapes=[
             pltpu.VMEM((rows, slots, 128), BF16),
             pltpu.VMEM((rows, slots, 128), BF16),
+            pltpu.SMEM(lens.shape, jnp.int32),
             pltpu.VMEM((rows, d_model), BF16),
+            pltpu.VMEM((d_model // 128, 128), BF16),
             pltpu.VMEM((d_model, 3 * width), BF16),
             pltpu.VMEM((width, d_model), BF16),
             pltpu.VMEM((rows * heads, 128), F32),
             pltpu.VMEM((rows * 8, 128), F32),
             pltpu.VMEM((rows * 8, 128), F32),
             pltpu.VMEM((rows * heads, 128), F32),
-            pltpu.SemaphoreType.DMA((5,)),
+            pltpu.SemaphoreType.DMA((7,)),
             pltpu.SemaphoreType.DMA((2, steps)),
-            pltpu.SemaphoreType.DMA((2, steps)),
+            pltpu.SemaphoreType.DMA((2,)),
         ],
         compiler_params=pltpu.CompilerParams(vmem_limit_bytes=63 << 20),
         cost_estimate=pl.CostEstimate(flops=400_000_000, bytes_accessed=42_000_000, transcendentals=0),
     )(lens, x, g.reshape(-1, 128), wq, wk, wv, wo, kc, vc)
 
 
-def experts_kernel(part_hbm, x_hbm, g_ref, picks, wr_hbm, wg, wu, wd, out_hbm,
-                   part, x_ref, wr, lsem, osem, gbuf, ubuf, dbuf, xf, recv1, hall, hb, gall, gt, z, acc, drecv, psum, frecv, yall,
+def experts_kernel(part_hbm, x_hbm, g_hbm, picks_hbm, wr_hbm, wg, wu, wd, out_hbm,
+                   part, x_ref, g_ref, picks, wr, lsem, osem, gbuf, ubuf, dbuf, xf, recv1, hall, hb, gall, gt, z, acc, drecv, psum, frecv, yall,
                    gsem, usem, dsem, s1, r1, s2, r2, s3, r3, s4, r4, s5, r5, s6, r6, s7, r7, s8, r8,
                    *, n_dp, n_tp, n_exp, ring, batch, chunks):
     dp = lax.axis_index("dp")
@@ -252,13 +251,11 @@
     for dev in peers + [partner, cross]:
         pl.semaphore_signal(barrier, inc=1, device_id=dev, device_id_type=MESH)
     loads = [pltpu.make_async_copy(a, b, lsem.at[i])
-             for i, (a, b) in enumerate(((part_hbm, part), (x_hbm, x_ref), (wr_hbm, wr)))]
+             for i, (a, b) in enumerate(((part_hbm, part), (x_hbm, x_ref), (g_hbm, g_ref),
+                                     (picks_hbm, picks), (wr_hbm, wr)))]
     for cp in loads:
         cp.start()
-    for cp in loads:
-        cp.wait()
-    start(0)
-    xf[...] = x_ref[...].astype(F32)
+    loads[0].wait()
     pl.semaphore_wait(barrier, len(peers) + 2)
 
     def block(t):
@@ -274,7 +271,11 @@
         cp.start()
         first.append(cp)
 
+    for cp in loads[1:]:
+        cp.wait()
+    start(0)
     start(1)
+    xf[...] = x_ref[...].astype(F32)
     pick_cols = []
     row8 = lax.broadcasted_iota(jnp.int32, (8, 128), 0)
     for kk in range(picks.shape[0]):
@@ -293,19 +294,22 @@
     h2 = norm_rows(x1, gain_row(g_ref))
     hall[me] = h2
 
+    def wait_all(ref, sem):
+        pltpu.make_async_copy(ref, ref, sem).wait()
+
     def spread(buf, i, m, ssem, rsem):
         return pltpu.make_async_remote_copy(
-            src_ref=buf.at[i], dst_ref=buf.at[i], send_sem=ssem.at[m], recv_sem=rsem.at[m],
+            src_ref=buf.at[i], dst_ref=buf.at[i], send_sem=ssem, recv_sem=rsem,
             device_id=peers[m], device_id_type=MESH)
 
     def relay(buf, i, m, ssem, rsem):
         return pltpu.make_async_remote_copy(
-            src_ref=buf.at[i], dst_ref=buf.at[i], send_sem=ssem.at[m], recv_sem=rsem.at[m],
+            src_ref=buf.at[i], dst_ref=buf.at[i], send_sem=ssem, recv_sem=rsem,
             device_id=partner, device_id_type=MESH)
 
     order = sorted(range(n_chip - 1), key=lambda m: -bin(m + 1).count("1"))
-    hs = [spread(hall, me, m, s2, r2) for m in range(n_chip - 1)]
-    hd = [relay(hall, me, n_chip - 1, s3, r3)]
+    hs = [spread(hall, me, m, s2.at[0], r2.at[m]) for m in range(n_chip - 1)]
+    hd = [relay(hall, me, n_chip - 1, s3.at[0], r3.at[0])]
     for m in order:
         hs[m].start()
     hd[0].start()
@@ -324,8 +328,8 @@
     for pc, ex in zip(pick_cols, exs):
         gates = gates + jnp.where(lane == pc, ex / den, 0.0)
     gall[me] = gates
-    gs = [spread(gall, me, m, s4, r4) for m in range(n_chip - 1)]
-    gd = [relay(gall, me, n_chip - 1, s5, r5)]
+    gs = [spread(gall, me, m, s4.at[0], r4.at[0]) for m in range(n_chip - 1)]
+    gd = [relay(gall, me, n_chip - 1, s5.at[0], r5.at[0])]
     for m in order:
         gs[m].start()
     gd[0].start()
@@ -336,11 +340,10 @@
 
     for m in reversed(order):
         hs[m].wait_recv()
-        cp = relay(hall, owner(m), m, s3, r3)
+        cp = relay(hall, owner(m), m, s3.at[0], r3.at[0])
         cp.start()
         hd.append(cp)
-    for cp in hd:
-        cp.wait_recv()
+    wait_all(hall.at[pl.ds(0, n_chip)], r3.at[0])
 
     for r in range(n_blk // 2):
         two = jnp.concatenate([hall[2 * r].astype(F32), hall[2 * r + 1].astype(F32)], axis=0)
@@ -376,14 +379,13 @@
     for b in range(len(batches)):
         now = products(b)
         if b == 0:
-            for m in reversed(order):
-                gs[m].wait_recv()
-                cp = relay(gall, owner(m), m, s5, r5)
+            wait_all(gall.at[pl.ds(0, n_chip - 1)], r4.at[0])
+            for m in order:
+                cp = relay(gall, owner(m), m, s5.at[0], r5.at[0])
                 cp.start()
                 gd.append(cp)
         if b == 1:
-            for cp in gd:
-                cp.wait_recv()
+            wait_all(gall.at[pl.ds(0, n_chip)], r5.at[0])
             gt[...] = gall[...].reshape(n_blk * 8, 128).T
         if before is not None:
             activate(b - 1, *before)
@@ -404,18 +406,19 @@
             chip = pd * (n_tp // 2) + px
             cp = pltpu.make_async_remote_copy(
                 src_ref=psum.at[n, block(chip)], dst_ref=frecv.at[n, m],
-                send_sem=s7.at[n, m], recv_sem=r7.at[n, m], device_id=peers[m], device_id_type=MESH)
+                send_sem=s7.at[0], recv_sem=r7.at[n], device_id=peers[m], device_id_type=MESH)
             cp.start()
             finals[n, m] = cp
 
     for n in range(chunks):
-        res = jnp.dot(z[...], dbuf[:, n * cw:(n + 1) * cw], preferred_element_type=F32)
+        cols = slice(n * cw, (n + 1) * cw)
+        res = jnp.dot(z[...], dbuf[:, cols], preferred_element_type=F32)
         for j in range(n_chip):
             for q in range(2):
                 at = (2 * j + q) * 8
                 acc[n, q, 8 * j:8 * j + 8, :] = res[at:at + 8, :]
         cp = pltpu.make_async_remote_copy(
-            src_ref=acc.at[n, 1 - core], dst_ref=drecv.at[n], send_sem=s6.at[n], recv_sem=r6.at[n],
+            src_ref=acc.at[n, 1 - core], dst_ref=drecv.at[n], send_sem=s6.at[0], recv_sem=r6.at[n],
             device_id=partner, device_id_type=MESH)
         cp.start()
         pair[n] = cp
@@ -423,33 +426,36 @@
             pair_sum(n - lag)
     for n in range(chunks - lag, chunks):
         pair_sum(n)
-    last = []
+    last, outs = [], []
     for n in range(chunks):
         total = psum[n, block(me_chip), :]
+        wait_all(frecv.at[n], r7.at[n])
         for m in range(n_chip - 1):
-            finals[n, m].wait_recv()
             total = total + frecv[n, m]
         cols = slice(n * cw, (n + 1) * cw)
-        yall[tp, :, cols] = (xf[block(tp), cols] + total).astype(BF16)
-        span = pl.ds(n * cw, cw)
+        yall[:, cols] = (xf[block(tp), cols] + total).astype(BF16)
+        if n % 2 == 0:
+            continue
+        span = pl.ds((n - 1) * cw, 2 * cw)
+        cp = pltpu.make_async_copy(yall.at[:, span], out_hbm.at[tp, :, span], osem.at[n // 2])
+        cp.start()
+        outs.append(cp)
         for k in (2, 1, 3):
             t_to = lax.rem(tp + k, n_tp)
             cp = pltpu.make_async_remote_copy(
-                src_ref=yall.at[tp, :, span], dst_ref=yall.at[tp, :, span],
-                send_sem=s8.at[n, k - 1], recv_sem=r8.at[n, k - 1],
+                src_ref=yall.at[:, span], dst_ref=out_hbm.at[tp, :, span],
+                send_sem=s8.at[0], recv_sem=r8.at[0],
                 device_id={"dp": dp, "tp": t_to}, device_id_type=MESH)
             cp.start()
             last.append(cp)
-    outs = []
-    for n in range(chunks):
-        span = pl.ds(n * cw, cw)
-        for cp in last[n * (n_tp - 1):(n + 1) * (n_tp - 1)]:
-            cp.wait_recv()
-        cp = pltpu.make_async_copy(yall.at[:, :, span], out_hbm.at[:, :, span], osem.at[n])
-        cp.start()
-        outs.append(cp)
-    for cp in hs + gs + hd + gd + list(pair.values()) + list(finals.values()) + last:
-        cp.wait_send()
+    wait_all(out_hbm.at[pl.ds(0, n_tp - 1)], r8.at[0])
+    wait_all(hall.at[pl.ds(0, n_chip - 1)], s2.at[0])
+    wait_all(hall.at[pl.ds(0, n_chip)], s3.at[0])
+    wait_all(gall.at[pl.ds(0, n_chip - 1)], s4.at[0])
+    wait_all(gall.at[pl.ds(0, n_chip)], s5.at[0])
+    wait_all(drecv, s6.at[0])
+    wait_all(frecv, s7.at[0])
+    wait_all(hall.at[pl.ds(0, n_tp - 1)], s8.at[0])
     for cp in outs:
         cp.wait()
 
@@ -469,13 +475,15 @@
                           chunks=chunks),
         name="experts",
         out_shape=jax.ShapeDtypeStruct((n_tp, 8, d_model), BF16),
-        in_specs=[ANY, ANY, VMEM, SMEM, ANY, ANY, ANY, ANY],
+        in_specs=[ANY] * 8,
         out_specs=ANY,
         scratch_shapes=[
             pltpu.VMEM((rows, d_model), F32),
             pltpu.VMEM((rows, d_model), BF16),
+            pltpu.VMEM((d_model // 128, 128), BF16),
+            pltpu.SMEM(picks.shape, jnp.int32),
             pltpu.VMEM(wr.shape, BF16),
-            dma((3,)), dma((chunks,)),
+            dma((5,)), dma((chunks // 2,)),
             pltpu.VMEM((ring, batch * f_dim, d_model), BF16),
             pltpu.VMEM((ring, batch * f_dim, d_model), BF16),
             pltpu.VMEM((mine * f_dim, d_model), BF16),
@@ -490,16 +498,16 @@
             pltpu.VMEM((chunks, n_chip * 8, cw), F32),
             pltpu.VMEM((chunks, n_chip * 8, cw), F32),
             pltpu.VMEM((chunks, n_chip - 1, 8, cw), F32),
-            pltpu.VMEM((n_tp, 8, d_model), BF16),
+            pltpu.VMEM((8, d_model), BF16),
             dma((ring,)), dma((ring,)), dma((n_batch,)),
             dma((n_tp - 1,)), dma((n_tp - 1,)),
-            dma((n_chip - 1,)), dma((n_chip - 1,)),
-            dma((n_chip,)), dma((n_chip,)),
-            dma((n_chip - 1,)), dma((n_chip - 1,)),
-            dma((n_chip,)), dma((n_chip,)),
-            dma((chunks,)), dma((chunks,)),
-            dma((chunks, n_chip - 1)), dma((chunks, n_chip - 1)),
-            dma((chunks, n_tp - 1)), dma((chunks, n_tp - 1)),
+            dma((1,)), dma((n_chip - 1,)),
+            dma((1,)), dma((1,)),
+            dma((1,)), dma((1,)),
+            dma((1,)), dma((1,)),
+            dma((1,)), dma((chunks,)),
+            dma((1,)), dma((chunks,)),
+            dma((1,)), dma((1,)),
         ],
         compiler_params=pltpu.CompilerParams(
             collective_id=0, has_side_effects=True, vmem_limit_bytes=63 << 20),

time: 61.7 us -> 57.3 us (0.929)
  Pallas kernels: 59.2 us -> 55 us
    pallas_call x1, Pallas kernels: 43.4 us -> 40.9 us  [experts(): pl.pallas_call(functools.partial(experts_kernel, n_dp=n_dp, n_tp=n_tp, n_...]
    pallas_call x1, Pallas kernels: 15.8 us -> 14.1 us  [attention(): pl.pallas_call(functools.partial(attention_kernel, group=group), name='at...]
where the time goes in v4:
time: 57.3 us; the launch traced here: 57.2 us
  Pallas kernels  55 us (96%)
  local copies, waits for them, and re-layouts  1.57 us (3%)
  between operations  0.65 us (1%)
    pallas_call x1, Pallas kernels, experts(): pl.pallas_call(functools.partial(experts_kernel, n_dp=n_dp, n_tp=n_tp, n_...  40.9 us
    pallas_call x1, Pallas kernels, attention(): pl.pallas_call(functools.partial(attention_kernel, group=group), name='at...  14.1 us
    unnamed x1, local copies, waits for them, and re-layouts  1.57 us

profile of v4, /device:TPU:0, one launch (start us, length us, event | category | flops | bytes accessed | tf_op | source)
XLA Modules:
  0.0 57.2 jit_solution(17370915241138661398)
XLA Ops:
  0.6 14.1 %attention.1 = (f32[32,2048]{1,0:T(8,128)}, bf16[32,1024,128]{2,1,0:T(8,128)(2,1)}, bf16[32,1024,128]{2,1,0:T(8,128)(2,1)}) custom-call(s32[32]{0:T(128)} %lens_hbm.1, bf16[32,2048]{1,0:T(8,128)(2,1)} %x_hbm.3, bf16[16,128]{1,0:T(8,128)(2,1)} %bitcast.20, bf16[2048,512]{1,0:T(8,128)(2,1)} %wq.1, bf16[2048,512]{1,0:T(8,128)(2,1)} %wk.1, ...), custom_call_target="tpu_custom_call" | custom-call | flops 400000000 | bytes 42000000 | tf_op jit(solution)/shard_map/attention/pallas_call | solution.py:171
  14.7 40.9 %experts.1 = bf16[4,8,2048]{2,1,0:T(8,128)(2,1)} custom-call(f32[32,2048]{1,0:T(8,128)} %get-tuple-element.6.part_hbm, bf16[32,2048]{1,0:T(8,128)(2,1)} %x_hbm.3, bf16[16,128]{1,0:T(8,128)(2,1)} %bitcast.21, s32[4,32]{1,0:T(4,128)} %bitcast.22, bf16[60,2048]{1,0:T(8,128)(2,1)} %bitcast.19, bf16[21120,2048]{1,0:T(8,128)(2,1)} %bitcast.7.wg, ...), custom_call_target="tpu_custom_call" | custom-call | flops 8000000000 | bytes 66000000 | tf_op jit(solution)/shard_map/experts/pallas_call | solution.py:473
  55.6 1.6 %copy.19 = bf16[32,2048]{1,0:T(8,128)(2,1)} copy(bf16[32,2048]{1,0:T(8,128)(2,1)} %bitcast.18) | data formatting | bytes 262144

commit v5 on v4

--- a/solution.py
+++ b/solution.py
@@ -338,7 +338,7 @@
         pd, px = chip_peer(m + 1)
         return pd * n_tp + 2 * px + core
 
-    for m in reversed(order):
+    for m in order:
         hs[m].wait_recv()
         cp = relay(hall, owner(m), m, s3.at[0], r3.at[0])
         cp.start()
@@ -434,10 +434,8 @@
             total = total + frecv[n, m]
         cols = slice(n * cw, (n + 1) * cw)
         yall[:, cols] = (xf[block(tp), cols] + total).astype(BF16)
-        if n % 2 == 0:
-            continue
-        span = pl.ds((n - 1) * cw, 2 * cw)
-        cp = pltpu.make_async_copy(yall.at[:, span], out_hbm.at[tp, :, span], osem.at[n // 2])
+        span = pl.ds(n * cw, cw)
+        cp = pltpu.make_async_copy(yall.at[:, span], out_hbm.at[tp, :, span], osem.at[n])
         cp.start()
         outs.append(cp)
         for k in (2, 1, 3):
@@ -483,7 +481,7 @@
             pltpu.VMEM((d_model // 128, 128), BF16),
             pltpu.SMEM(picks.shape, jnp.int32),
             pltpu.VMEM(wr.shape, BF16),
-            dma((5,)), dma((chunks // 2,)),
+            dma((5,)), dma((chunks,)),
             pltpu.VMEM((ring, batch * f_dim, d_model), BF16),
             pltpu.VMEM((ring, batch * f_dim, d_model), BF16),
             pltpu.VMEM((mine * f_dim, d_model), BF16),

time: 57.3 us -> 57.4 us (level)
  no operation moved by 1% of the time
where the time goes in v5:
time: 57.4 us; the launch traced here: 57.3 us
  Pallas kernels  55.1 us (96%)
  local copies, waits for them, and re-layouts  1.57 us (3%)
  between operations  0.65 us (1%)
    pallas_call x1, Pallas kernels, experts(): pl.pallas_call(functools.partial(experts_kernel, n_dp=n_dp, n_tp=n_tp, n_...  41 us
    pallas_call x1, Pallas kernels, attention(): pl.pallas_call(functools.partial(attention_kernel, group=group), name='at...  14.1 us
    unnamed x1, local copies, waits for them, and re-layouts  1.57 us

profile of v5, /device:TPU:0, one launch (start us, length us, event | category | flops | bytes accessed | tf_op | source)
XLA Modules:
  0.0 57.3 jit_solution(7055862501300575203)
XLA Ops:
  0.6 14.1 %attention.1 = (f32[32,2048]{1,0:T(8,128)}, bf16[32,1024,128]{2,1,0:T(8,128)(2,1)}, bf16[32,1024,128]{2,1,0:T(8,128)(2,1)}) custom-call(s32[32]{0:T(128)} %lens_hbm.1, bf16[32,2048]{1,0:T(8,128)(2,1)} %x_hbm.3, bf16[16,128]{1,0:T(8,128)(2,1)} %bitcast.20, bf16[2048,512]{1,0:T(8,128)(2,1)} %wq.1, bf16[2048,512]{1,0:T(8,128)(2,1)} %wk.1, ...), custom_call_target="tpu_custom_call" | custom-call | flops 400000000 | bytes 42000000 | tf_op jit(solution)/shard_map/attention/pallas_call | solution.py:171
  14.7 41.0 %experts.1 = bf16[4,8,2048]{2,1,0:T(8,128)(2,1)} custom-call(f32[32,2048]{1,0:T(8,128)} %get-tuple-element.6.part_hbm, bf16[32,2048]{1,0:T(8,128)(2,1)} %x_hbm.3, bf16[16,128]{1,0:T(8,128)(2,1)} %bitcast.21, s32[4,32]{1,0:T(4,128)} %bitcast.22, bf16[60,2048]{1,0:T(8,128)(2,1)} %bitcast.19, bf16[21120,2048]{1,0:T(8,128)(2,1)} %bitcast.7.wg, ...), custom_call_target="tpu_custom_call" | custom-call | flops 8000000000 | bytes 66000000 | tf_op jit(solution)/shard_map/experts/pallas_call | solution.py:471
  55.7 1.6 %copy.19 = bf16[32,2048]{1,0:T(8,128)(2,1)} copy(bf16[32,2048]{1,0:T(8,128)(2,1)} %bitcast.18) | data formatting | bytes 262144
